TPU v7x, 32 devices: a 4x4x1 block of a 4x4x8 slice. The times are simulated.
32 devices in a mesh: replica: 1 (over z), heads: 4 (over y), model: 8 (over x, core).
Axes of the slice: x: 4, y: 4, z: 1, core: 2. Of those that a mesh axis runs over, the one named last changes fastest.
The devices are a block of a 4x4x8 slice.
Arguments:
- tokens: bfloat16 [256, 8192], P('replica')
- w_query: bfloat16 [8192, 8192], P(None, ('heads', 'model'))
- w_key: bfloat16 [8192, 1024], replicated
- w_value: bfloat16 [8192, 1024], replicated
- w_out: bfloat16 [8192, 8192], P(('heads', 'model'))
- key_cache: bfloat16 [256, 8, 1024, 128], P(('replica', 'model'))
- value_cache: bfloat16 [256, 8, 1024, 128], P(('replica', 'model'))
- lengths: int32 [256], P(('replica', 'model'))
Outputs:
- output 1: bfloat16 [256, 8192], P('replica')
- output 2: bfloat16 [256, 8, 128], P(('replica', 'model'))
- output 3: bfloat16 [256, 8, 128], P(('replica', 'model'))
All inputs are finite; a program needn't handle non-finite values.
Results may differ from a plain program's by a relative error of at most 0.002.
Values are sent between devices in bfloat16 or wider.
A program may use at most 768 MiB of HBM per device.

v0:
```python
import jax
import jax.numpy as jnp
from jax import lax
from jax.sharding import PartitionSpec as P


def attend(queries, key_rows, value_rows, key_last, value_last, seq_len):
    score_scale = queries.shape[-1] ** -0.5
    scores = jnp.einsum("bgrd,bgtd->bgrt", queries, key_rows, preferred_element_type=jnp.float32) * score_scale
    score_new = jnp.einsum("bgrd,bgd->bgr", queries, key_last, preferred_element_type=jnp.float32) * score_scale
    positions = lax.broadcasted_iota(jnp.int32, (1, 1, 1, key_rows.shape[2]), 3)
    scores = jnp.where(positions < seq_len[:, None, None, None], scores, -jnp.inf)
    score_max = jnp.maximum(jnp.max(scores, axis=-1), score_new)
    weights = jnp.exp(scores - score_max[..., None])
    weight_new = jnp.exp(score_new - score_max)
    denom_sum = jnp.sum(weights, axis=-1) + weight_new
    weighted_sum = jnp.einsum("bgrt,bgtd->bgrd", weights.astype(jnp.bfloat16), value_rows, preferred_element_type=jnp.float32)
    weighted_sum = weighted_sum + weight_new.astype(jnp.bfloat16).astype(jnp.float32)[..., None] * value_last.astype(jnp.float32)[:, :, None, :]
    return (weighted_sum / denom_sum[..., None]).astype(jnp.bfloat16)


def solution(mesh):
    heads_count = mesh.shape["heads"]
    model_count = mesh.shape["model"]

    def local_step(tokens, w_query, w_key, w_value, w_out, key_cache, value_cache, lengths):
        batch_all = tokens.shape[0]
        local_rows = key_cache.shape[0]
        kv_count = key_cache.shape[1]
        head_dim = key_cache.shape[3]
        heads_local = w_query.shape[1] // head_dim
        heads_shard = heads_local * model_count
        group_size = heads_shard * heads_count // kv_count
        shard_groups = max(1, heads_shard // group_size)
        head_index = lax.axis_index("heads")
        model_index = lax.axis_index("model")
        queries = jnp.dot(tokens, w_query, preferred_element_type=jnp.float32).astype(jnp.bfloat16)
        queries = lax.all_to_all(queries.reshape(batch_all, heads_local, head_dim), "model", 0, 1, tiled=True)
        own_tokens = lax.dynamic_slice_in_dim(tokens, model_index * local_rows, local_rows, 0)
        key_new = jnp.dot(own_tokens, w_key, preferred_element_type=jnp.float32).astype(jnp.bfloat16)
        key_new = key_new.reshape(local_rows, kv_count, head_dim)
        value_new = jnp.dot(own_tokens, w_value, preferred_element_type=jnp.float32).astype(jnp.bfloat16)
        value_new = value_new.reshape(local_rows, kv_count, head_dim)
        first_group = head_index * heads_shard // group_size
        attended = attend(
            queries.reshape(local_rows, shard_groups, heads_shard // shard_groups, head_dim),
            lax.dynamic_slice_in_dim(key_cache, first_group, shard_groups, 1),
            lax.dynamic_slice_in_dim(value_cache, first_group, shard_groups, 1),
            lax.dynamic_slice_in_dim(key_new, first_group, shard_groups, 1),
            lax.dynamic_slice_in_dim(value_new, first_group, shard_groups, 1),
            lengths,
        )
        attended = lax.all_to_all(attended.reshape(local_rows, heads_shard, head_dim), "model", 1, 0, tiled=True)
        partial = jnp.dot(attended.reshape(batch_all, heads_local * head_dim), w_out, preferred_element_type=jnp.float32)
        mixed_sum = lax.psum(partial, ("heads", "model"))
        out_tokens = (tokens.astype(jnp.float32) + mixed_sum).astype(jnp.bfloat16)
        return (out_tokens, key_new, value_new)

    cache_spec = P(("replica", "model"), None, None, None)
    new_spec = P(("replica", "model"), None, None)
    return jax.shard_map(
        local_step,
        mesh=mesh,
        in_specs=(P("replica", None), P(None, ("heads", "model")), P(None, None), P(None, None), P(("heads", "model"), None), cache_spec, cache_spec, P(("replica", "model"))),
        out_specs=(P("replica", None), new_spec, new_spec),
        check_vma=False,
    )
```

profile of v0, /device:TPU:97, one launch (start us, length us, event | category | flops | bytes accessed | tf_op | source)
XLA Modules:
  0.0 191.1 jit_solution(14668932281544206243)
XLA Ops:
  7.2 0.0 copy-start.4
  7.2 5.2 %convolution_convert_fusion = bf16[256,256]{0,1:T(8,128)(2,1)S(1)} fusion(bf16[256,8192]{1,0:T(8,128)(2,1)} %param.8, bf16[8192,256]{1,0:T(8,128)(2,1)} %param.9), kind=kOutput, calls=%fused_computation.11 | convolution fusion | flops 1073807360 | bytes 8519680 | tf_op jit(solution)/shard_map/dot_general | solution.py:37
  12.4 0.8 copy.18
  13.2 6.0 %all-to-all-start = ((bf16[256,2,128]{2,1,0:T(2,128)(2,1)}), bf16[256,2,128]{2,1,0:T(2,128)(2,1)S(1)}, u32[]{:S(2)}, u32[]{:S(2)}) async-start(bf16[256,2,128]{2,1,0:T(2,128)(2,1)} %copy.18), calls=%async_computation | async-start | bytes 262144 | tf_op jit(solution)/shard_map/all_to_all | solution.py:38
  19.2 0.0 all-reduce.2.cloned.1.call-start
  19.2 0.0 copy-done.4
  19.2 0.1 iota_compare_fusion
  19.3 0.0 copy-start
  19.3 9.1 %fusion.10 = bf16[4,8,8,128]{3,1,2,0:T(8,128)(2,1)S(1)} fusion(bf16[8192,1024]{1,0:T(8,128)(2,1)} %param.10, bf16[256,8192]{1,0:T(8,128)(2,1)} %param.8, s32[]{:T(128)S(6)} %select_n.21), kind=kOutput, calls=%fused_computation.14 | convolution fusion | flops 536903680 | bytes 17367044 | tf_op jit(solution)/shard_map/dot_general | solution.py:40
  28.4 1.6 copy-done
  30.0 0.0 copy-start.2
  30.0 4.1 %fusion.11 = bf16[4,8,8,128]{3,1,2,0:T(8,128)(2,1)S(1)} fusion(bf16[8192,1024]{1,0:T(8,128)(2,1)S(1)} %copy-done, bf16[256,8192]{1,0:T(8,128)(2,1)} %param.8, s32[]{:T(128)S(6)} %select_n.21), kind=kOutput, calls=%fused_computation.15 | convolution fusion | flops 536903680 | bytes 17367044 | tf_op jit(solution)/shard_map/dot_general | solution.py:42
  34.1 0.0 copy-done.2
  34.2 0.0 copy-start.3
  34.2 0.0 all-to-all-done
  34.2 0.1 copy.20
  34.4 0.2 fusion.31
  34.6 8.2 %fusion.4 = (f32[32,2,8]{2,1,0:T(2,128)S(1)}, f32[32,2,8,1024]{3,2,1,0:T(8,128)S(1)}) fusion(pred[32,1024]{1,0:T(8,128)(4,1)S(1)} %iota_compare_fusion, bf16[32,2,8,128]{3,2,1,0:T(8,128)(2,1)S(1)} %bitcast.33, bf16[32,8,1024,128]{3,2,1,0:T(8,128)(2,1)} %param.13, s32[]{:T(128)S(6)} %select_n.19), kind=kOutput, calls=%fused_computation.7 | convolution fusion | flops 135790080 | bytes 19040260 | tf_op jit(solution)/shard_map/bgrd,bgtd->bgrt/dot_general | solution.py:9
  42.8 0.0 copy-done.3
  42.8 0.7 fusion.5
  43.5 0.0 copy-start.1
  43.5 7.4 %fusion.18 = bf16[32,16,128]{2,1,0:T(8,128)(2,1)S(1)} fusion(bf16[32,8,1024,128]{3,2,1,0:T(8,128)(2,1)} %param.14, s32[]{:T(128)S(6)} %select_n.19, f32[32,2,8,1024]{3,2,1,0:T(8,128)S(1)} %get-tuple-element.6, f32[32,2,8]{2,1,0:T(2,128)S(1)} %multiply_maximum_fusion, pred[32,1024]{1,0:T(8,128)(4,1)S(1)} %iota_compare_fusion, ...), kind=kOutput, calls=%fused_computation.18 | convolution fusion | flops 136577024 | bytes 19077124 | tf_op jit(solution)/shard_map/bgrt,bgtd->bgrd/dot_general | solution.py:17
  51.0 9.9 %all_to_all.30 = bf16[32,16,128]{2,0,1:T(8,128)(2,1)S(1)} all-to-all(bf16[32,16,128]{2,0,1:T(8,128)(2,1)S(1)} %copy.21), channel_id=1, replica_groups=mesh['replica'=1,'heads'=4,'model'=8] {'model'}, dimensions={1} | all-to-all | bytes 262144 | tf_op jit(solution)/shard_map/all_to_all | solution.py:53
  60.8 0.1 copy.22
  61.0 0.0 copy-done.1
  61.0 4.5 %fusion.28 = f32[256,8192]{1,0:T(8,128)} fusion(bf16[256,8192]{1,0:T(8,128)(2,1)S(1)} %copy-done.1, bf16[32,8,2,128]{3,2,1,0:T(2,128)(2,1)S(1)} %bitcast.34), kind=kOutput, calls=%fused_computation.25 | convolution fusion | flops 1073741824 | bytes 12713984 | tf_op jit(solution)/shard_map/dot_general | solution.py:54
  65.5 0.1 all-reduce.2.cloned.1.call-update
  65.5 111.0 %all-reduce.2.cloned.1.call-done = f32[256,8192]{1,0:T(8,128)} async-done(((f32[256,8192]{1,0:T(8,128)}), f32[256,8192]{1,0:T(8,128)}) %all-reduce.2.cloned.1.call-update) | async-done | bytes 8388624 | tf_op jit(solution)/shard_map/psum | solution.py:55
  176.5 7.7 %add_convert_fusion = bf16[256,8192]{1,0:T(8,128)(2,1)} fusion(f32[256,8192]{1,0:T(8,128)} %all-reduce.2.cloned.1.call-done, bf16[256,8192]{1,0:T(8,128)(2,1)} %param.8), kind=kLoop, calls=%fused_computation.4 | loop fusion | flops 6291456 | bytes 16777216 | tf_op jit(solution)/shard_map/convert_element_type | solution.py:56
  (8 shorter events, 0.2 us)
Async XLA Ops:
  7.2 12.0 %copy-start.4 = (s32[32]{0:T(128)S(1)}, s32[32]{0:T(128)}, u32[]{:S(2)}) copy-start(s32[32]{0:T(128)} %param.15) | copy-start | bytes 388
  13.2 21.0 %all-to-all-start = ((bf16[256,2,128]{2,1,0:T(2,128)(2,1)}), bf16[256,2,128]{2,1,0:T(2,128)(2,1)S(1)}, u32[]{:S(2)}, u32[]{:S(2)}) async-start(bf16[256,2,128]{2,1,0:T(2,128)(2,1)} %copy.18), calls=%async_computation | async-start | bytes 262144 | tf_op jit(solution)/shard_map/all_to_all | solution.py:38
  19.2 157.3 %all-reduce.2.cloned.1.call-start = ((), (), s32[]{:S(2)}) async-start(), calls=%async_computation.2 | async-start | bytes 16777216 | tf_op jit(solution)/shard_map/psum | solution.py:55
  19.3 10.7 %copy-start = (bf16[8192,1024]{1,0:T(8,128)(2,1)S(1)}, bf16[8192,1024]{1,0:T(8,128)(2,1)}, u32[]{:S(2)}) copy-start(bf16[8192,1024]{1,0:T(8,128)(2,1)} %param.11) | copy-start | bytes 50331652
  30.0 4.1 %copy-start.2 = (bf16[4,8,8,128]{3,2,1,0:T(8,128)(2,1)}, bf16[4,8,8,128]{3,2,1,0:T(8,128)(2,1)S(1)}, u32[]{:S(2)}) copy-start(bf16[4,8,8,128]{3,2,1,0:T(8,128)(2,1)S(1)} %copy.25) | copy-start | bytes 196612
  34.2 8.6 %copy-start.3 = (bf16[4,8,8,128]{3,2,1,0:T(8,128)(2,1)}, bf16[4,8,8,128]{3,2,1,0:T(8,128)(2,1)S(1)}, u32[]{:S(2)}) copy-start(bf16[4,8,8,128]{3,2,1,0:T(8,128)(2,1)S(1)} %copy.26) | copy-start | bytes 196612
  43.5 17.4 %copy-start.1 = (bf16[256,8192]{1,0:T(8,128)(2,1)S(1)}, bf16[256,8192]{1,0:T(8,128)(2,1)}, u32[]{:S(2)}) copy-start(bf16[256,8192]{1,0:T(8,128)(2,1)} %param.12) | copy-start | bytes 12582916
Sparse Core Ops, SparseCore 0:
  65.6 110.8 all-reduce.1
where the time goes:
time: 191 us
  waiting for transfers between devices  111 us (58%)
  matrix products  38.6 us (20%)
  between operations  14.2 us (7%)
  blocking collectives  9.86 us (5%)
  other arithmetic  8.54 us (4%)
  starting transfers between devices  6.02 us (3%)
  local copies, waits for them, and re-layouts  2.76 us (1%)
    psum x1, waiting for transfers between devices, local_step(): mixed_sum = lax.psum(partial, ('heads', 'model'))  111 us
    all_to_all x1, blocking collectives, local_step(): lax.all_to_all(attended.reshape(local_rows, heads_shard, head_dim), 'mode...  9.86 us
    dot_general x1, matrix products, local_step(): jnp.dot(own_tokens, w_key, preferred_element_type=jnp.float32)  9.06 us
    dot_general x1, matrix products, attend(): jnp.einsum('bgrd,bgtd->bgrt', queries, key_rows, preferred_element_type=j...  8.18 us
    convert_element_type x1, other arithmetic, local_step(): out_tokens = (tokens.astype(jnp.float32) + mixed_sum).astype(jnp.bfloat16)  7.69 us
    dot_general x1, matrix products, attend(): jnp.einsum('bgrt,bgtd->bgrd', weights.astype(jnp.bfloat16), value_rows, p...  7.4 us
    all_to_all x1, starting transfers between devices, local_step(): lax.all_to_all(queries.reshape(batch_all, heads_local, head_dim), 'model'...  6.01 us
    dot_general x1, matrix products, local_step(): jnp.dot(tokens, w_query, preferred_element_type=jnp.float32)  5.2 us
  transfers between devices with their start and end apart: 2, of which 1 were waited for; matrix products, arithmetic and copies ran while one was open for 7% of the time, Pallas kernels for 0%

commit v1 on v0

--- a/solution.py
+++ b/solution.py
@@ -1,7 +1,15 @@
+import functools
+
 import jax
 import jax.numpy as jnp
 from jax import lax
+from jax.experimental import pallas as pl
+from jax.experimental.pallas import tpu as pltpu
 from jax.sharding import PartitionSpec as P
+
+MESH = pl.DeviceIdType.MESH
+CHUNKS = 2
+OFFSET = 2
 
 
 def attend(queries, key_rows, value_rows, key_last, value_last, seq_len):
@@ -17,6 +25,299 @@
     weighted_sum = jnp.einsum("bgrt,bgtd->bgrd", weights.astype(jnp.bfloat16), value_rows, preferred_element_type=jnp.float32)
     weighted_sum = weighted_sum + weight_new.astype(jnp.bfloat16).astype(jnp.float32)[..., None] * value_last.astype(jnp.float32)[:, :, None, :]
     return (weighted_sum / denom_sum[..., None]).astype(jnp.bfloat16)
+
+
+def mix_kernel(ny, nx, o_ref, wo_ref, tok_ref, out_ref,
+               w_buf, o_all, part, recv1, recv2, tok_buf,
+               o_send, o_recv, w_sem, tok_sem, sems1, sems2, sems3, sems4, sems_d):
+    y = lax.axis_index("heads")
+    model = lax.axis_index("model")
+    x = lax.div(model, 2)
+    core = lax.rem(model, 2)
+    rows = o_ref.shape[1]
+    depth = wo_ref.shape[0]
+    cols = wo_ref.shape[1] // 2
+    half = cols // 2
+    block = half // 4
+    r = rows // CHUNKS
+    groups = 2 * nx
+
+    def dev(yy, xx, cc):
+        return {"heads": lax.rem(yy + ny, ny), "model": 2 * lax.rem(xx + nx, nx) + cc}
+
+    partner = dev(y, x, 1 - core)
+    x_next, x_prev = dev(y, x + 1, core), dev(y, x - 1, core)
+    y_next, y_prev = dev(y + 1, x, core), dev(y - 1, x, core)
+
+    barrier = pltpu.get_barrier_semaphore()
+    peers = [partner, y_next, y_prev]
+    for step in range(1, nx):
+        for cc in range(2):
+            peers.append(dev(y, x + step, cc))
+    for peer in peers:
+        pl.semaphore_signal(barrier, inc=1, device_id=peer, device_id_type=MESH)
+    my_cols = pl.ds(pl.multiple_of(core * cols, cols), cols)
+    other_cols = pl.ds(pl.multiple_of((1 - core) * cols, cols), cols)
+    my_rows = pl.ds(pl.multiple_of(core * depth, depth), depth)
+    own_w = pltpu.make_async_copy(wo_ref.at[:, my_cols], w_buf.at[my_rows], w_sem.at[2])
+    own_w.start()
+    pos1 = (x, y)
+    pos2 = (y, x)
+    tok_copies = []
+    for h in range(2):
+        c0 = pl.multiple_of(core * cols + h * half + pos1[h] * block, block)
+        copy = pltpu.make_async_copy(tok_ref.at[pl.ds(2 * pos2[h], 2), :, pl.ds(c0, block)], tok_buf.at[h], tok_sem.at[h])
+        copy.start()
+        tok_copies.append(copy)
+    pl.semaphore_wait(barrier, len(peers))
+
+    o_copies = []
+    n = 0
+    for step in [1, nx - 1] + list(range(2, nx - 1)) + [0]:
+        for cc in range(2):
+            tx = lax.rem(x + step, nx)
+            if step == 0:
+                if cc == 1:
+                    continue
+                target = partner
+            else:
+                target = dev(y, x + step, cc)
+            copy = pltpu.make_async_remote_copy(
+                src_ref=o_ref.at[tx], dst_ref=o_all.at[model],
+                send_sem=o_send.at[n],
+                recv_sem=o_recv.at[(nx - step) % nx * 2 + core if step else 2 * 0],
+                device_id=target, device_id_type=MESH)
+            copy.start()
+            o_copies.append(copy)
+            n += 1
+    w_copy = pltpu.make_async_remote_copy(
+        src_ref=wo_ref.at[:, other_cols], dst_ref=w_buf.at[my_rows],
+        send_sem=w_sem.at[0], recv_sem=w_sem.at[1], device_id=partner, device_id_type=MESH)
+    w_copy.start()
+    o_all[pl.ds(model, 1)] = o_ref[pl.ds(x, 1)]
+
+    def wait_recv(dst, sem):
+        pltpu.make_async_copy(dst, dst, sem).wait()
+
+    for step in range(1, nx):
+        for cc in range(2):
+            source = 2 * lax.rem(x + step, nx) + cc
+            wait_recv(o_all.at[source], o_recv.at[step * 2 + cc])
+    wait_recv(o_all.at[2 * x + 1 - core], o_recv.at[0])
+    own_w.wait()
+    w_copy.wait_recv()
+    for copy in tok_copies:
+        copy.wait()
+
+    sends = list(o_copies)
+
+    def remote(src, dst, sems, index, target):
+        copy = pltpu.make_async_remote_copy(
+            src_ref=src, dst_ref=dst, send_sem=sems.at[0, index], recv_sem=sems.at[1, index],
+            device_id=target, device_id_type=MESH)
+        copy.start()
+        sends.append(copy)
+        return copy
+
+    nexts = ((x_next, y_next), (y_next, x_next))
+    prevs = ((x_prev, y_prev), (y_prev, x_prev))
+    flows = {}
+    hg = groups // 2
+
+    def base(h):
+        return h * half
+
+    def cols_of(h, d):
+        return pl.ds(pl.multiple_of(base(h) + lax.rem(d + 4, 4) * block, block), block)
+
+    def compute(k, h, d):
+        lhs = o_all[:, k * r:(k + 1) * r, :].reshape(groups * r, o_all.shape[2])
+        acc = jnp.dot(lhs, w_buf[:, cols_of(h, d)], preferred_element_type=jnp.float32)
+        part[k, :, :, cols_of(h, d)] = acc.reshape(groups, r, block)
+
+    def sidx(k, h, i):
+        return (k * 2 + h) * 6 + i
+
+    def s0(k):
+        for h in range(2):
+            p = pos1[h]
+            compute(k, h, p + 2)
+            c = cols_of(h, p + 2)
+            flows[k, h, 0] = remote(part.at[k, 0:hg, :, c], recv1.at[k, h, 0], sems1, sidx(k, h, 0), nexts[h][0])
+            flows[k, h, 1] = remote(part.at[k, hg:groups, :, c], recv1.at[k, h, 1], sems1, sidx(k, h, 1), prevs[h][0])
+        for h in range(2):
+            p = pos1[h]
+            compute(k, h, p + 1)
+            flows[k, h, 2] = remote(part.at[k, hg:groups, :, cols_of(h, p + 1)], recv1.at[k, h, 2], sems1, sidx(k, h, 2), nexts[h][0])
+            compute(k, h, p - 1)
+            flows[k, h, 3] = remote(part.at[k, 0:hg, :, cols_of(h, p - 1)], recv1.at[k, h, 3], sems1, sidx(k, h, 3), prevs[h][0])
+        for h in range(2):
+            compute(k, h, pos1[h])
+
+    def s1(k):
+        for h in range(2):
+            p = pos1[h]
+            c = cols_of(h, p + 1)
+            flows[k, h, 0].wait_recv()
+            part[k, 0:hg, :, c] = part[k, 0:hg, :, c] + recv1[k, h, 0]
+            flows[k, h, 4] = remote(part.at[k, 0:hg, :, c], recv1.at[k, h, 4], sems1, sidx(k, h, 4), nexts[h][0])
+            c = cols_of(h, p - 1)
+            flows[k, h, 1].wait_recv()
+            part[k, hg:groups, :, c] = part[k, hg:groups, :, c] + recv1[k, h, 1]
+            flows[k, h, 5] = remote(part.at[k, hg:groups, :, c], recv1.at[k, h, 5], sems1, sidx(k, h, 5), prevs[h][0])
+
+    def s2(k):
+        for h in range(2):
+            c = cols_of(h, pos1[h])
+            q = pos2[h]
+            for i in (2, 3, 4, 5):
+                flows[k, h, i].wait_recv()
+            part[k, 0:hg, :, c] = part[k, 0:hg, :, c] + recv1[k, h, 3] + recv1[k, h, 4]
+            part[k, hg:groups, :, c] = part[k, hg:groups, :, c] + recv1[k, h, 2] + recv1[k, h, 5]
+            far, up, down = lax.rem(q + 2, 4), lax.rem(q + 1, 4), lax.rem(q + 3, 4)
+            flows[k, h, 10] = remote(part.at[k, 2 * far, :, c], recv2.at[k, h, 0], sems2, sidx(k, h, 0), nexts[h][1])
+            flows[k, h, 11] = remote(part.at[k, 2 * far + 1, :, c], recv2.at[k, h, 1], sems2, sidx(k, h, 1), prevs[h][1])
+            flows[k, h, 12] = remote(part.at[k, 2 * up + 1, :, c], recv2.at[k, h, 2], sems2, sidx(k, h, 2), nexts[h][1])
+            flows[k, h, 13] = remote(part.at[k, 2 * down, :, c], recv2.at[k, h, 3], sems2, sidx(k, h, 3), prevs[h][1])
+
+    def s3(k):
+        for h in range(2):
+            c = cols_of(h, pos1[h])
+            q = pos2[h]
+            up, down = lax.rem(q + 1, 4), lax.rem(q + 3, 4)
+            flows[k, h, 10].wait_recv()
+            part[k, 2 * up, :, c] = part[k, 2 * up, :, c] + recv2[k, h, 0]
+            flows[k, h, 14] = remote(part.at[k, 2 * up, :, c], recv2.at[k, h, 4], sems2, sidx(k, h, 4), nexts[h][1])
+            flows[k, h, 11].wait_recv()
+            part[k, 2 * down + 1, :, c] = part[k, 2 * down + 1, :, c] + recv2[k, h, 1]
+            flows[k, h, 15] = remote(part.at[k, 2 * down + 1, :, c], recv2.at[k, h, 5], sems2, sidx(k, h, 5), prevs[h][1])
+
+    def out_cols(h, d):
+        return pl.ds(pl.multiple_of(core * cols + base(h) + lax.rem(d + 4, 4) * block, block), block)
+
+    def region(k, g0, ng, c):
+        return out_ref.at[pl.ds(g0, ng), k * r:(k + 1) * r, c]
+
+    def aidx(k, h, i):
+        return (k * 2 + h) * 4 + i
+
+    def s4(k):
+        for h in range(2):
+            c = cols_of(h, pos1[h])
+            oc = out_cols(h, pos1[h])
+            q = pos2[h]
+            for i in (12, 13, 14, 15):
+                flows[k, h, i].wait_recv()
+            low = part[k, 2 * q, :, c] + recv2[k, h, 3] + recv2[k, h, 4]
+            high = part[k, 2 * q + 1, :, c] + recv2[k, h, 2] + recv2[k, h, 5]
+            low = tok_buf[h, 0, k * r:(k + 1) * r, :].astype(jnp.float32) + low
+            high = tok_buf[h, 1, k * r:(k + 1) * r, :].astype(jnp.float32) + high
+            out_ref[2 * q, k * r:(k + 1) * r, oc] = low.astype(out_ref.dtype)
+            out_ref[2 * q + 1, k * r:(k + 1) * r, oc] = high.astype(out_ref.dtype)
+            src = region(k, 2 * q, 2, oc)
+            flows[k, h, 20] = remote(src, src, sems3, aidx(k, h, 0), nexts[h][1])
+            flows[k, h, 21] = remote(src, src, sems3, aidx(k, h, 1), prevs[h][1])
+
+    def s5(k):
+        for h in range(2):
+            oc = out_cols(h, pos1[h])
+            q = pos2[h]
+            up, down = lax.rem(q + 1, 4), lax.rem(q + 3, 4)
+            wait_recv(region(k, 2 * down, 2, oc), sems3.at[1, aidx(k, h, 0)])
+            src = region(k, 2 * down, 1, oc)
+            flows[k, h, 22] = remote(src, src, sems3, aidx(k, h, 2), nexts[h][1])
+            wait_recv(region(k, 2 * up, 2, oc), sems3.at[1, aidx(k, h, 1)])
+            src = region(k, 2 * up + 1, 1, oc)
+            flows[k, h, 23] = remote(src, src, sems3, aidx(k, h, 3), prevs[h][1])
+
+    def didx(k, h, i):
+        return (k * 2 + h) * 5 + i
+
+    def s6(k):
+        for h in range(2):
+            oc = out_cols(h, pos1[h])
+            q = pos2[h]
+            far = lax.rem(q + 2, 4)
+            wait_recv(region(k, 2 * far, 1, oc), sems3.at[1, aidx(k, h, 2)])
+            wait_recv(region(k, 2 * far + 1, 1, oc), sems3.at[1, aidx(k, h, 3)])
+            src = region(k, 0, groups, oc)
+            flows[k, h, 30] = remote(src, src, sems4, aidx(k, h, 0), nexts[h][0])
+            flows[k, h, 31] = remote(src, src, sems4, aidx(k, h, 1), prevs[h][0])
+            remote(src, src, sems_d, didx(k, h, 0), partner)
+
+    def s7(k):
+        for h in range(2):
+            p = pos1[h]
+            down, up = out_cols(h, p - 1), out_cols(h, p + 1)
+            wait_recv(region(k, 0, groups, down), sems4.at[1, aidx(k, h, 0)])
+            src = region(k, 0, hg, down)
+            remote(src, src, sems4, aidx(k, h, 2), nexts[h][0])
+            wait_recv(region(k, 0, groups, up), sems4.at[1, aidx(k, h, 1)])
+            src = region(k, hg, hg, up)
+            remote(src, src, sems4, aidx(k, h, 3), prevs[h][0])
+            src = region(k, 0, groups, down)
+            remote(src, src, sems_d, didx(k, h, 1), partner)
+            src = region(k, 0, groups, up)
+            remote(src, src, sems_d, didx(k, h, 2), partner)
+
+    def s8(k):
+        for h in range(2):
+            far = out_cols(h, pos1[h] + 2)
+            for i in range(2):
+                src = region(k, i * hg, hg, far)
+                wait_recv(src, sems4.at[1, aidx(k, h, 2 + i)])
+                remote(src, src, sems_d, didx(k, h, 3 + i), partner)
+
+    stages = [s0, s1, s2, s3, s4, s5, s6, s7, s8]
+    for slot in range(len(stages) + OFFSET * (CHUNKS - 1)):
+        for k in range(CHUNKS):
+            if 0 <= slot - OFFSET * k < len(stages):
+                stages[slot - OFFSET * k](k)
+
+    def other_out_cols(h, d):
+        return pl.ds(pl.multiple_of((1 - core) * cols + base(h) + lax.rem(d + 4, 4) * block, block), block)
+
+    for k in range(CHUNKS):
+        for h in range(2):
+            p = pos1[h]
+            wait_recv(region(k, 0, groups, other_out_cols(h, p)), sems_d.at[1, didx(k, h, 0)])
+            wait_recv(region(k, 0, groups, other_out_cols(h, p - 1)), sems_d.at[1, didx(k, h, 1)])
+            wait_recv(region(k, 0, groups, other_out_cols(h, p + 1)), sems_d.at[1, didx(k, h, 2)])
+            for i in range(2):
+                wait_recv(region(k, i * hg, hg, other_out_cols(h, p + 2)), sems_d.at[1, didx(k, h, 3 + i)])
+    for copy in sends:
+        copy.wait_send()
+    w_copy.wait_send()
+
+
+def mix(ny, nx, o_parts, w_out, tokens):
+    groups = 2 * nx
+    rows = o_parts.shape[1]
+    width = w_out.shape[1]
+    cols = width // 2
+    block = cols // 8
+    r = rows // CHUNKS
+    any_spec = pl.BlockSpec(memory_space=pl.ANY)
+    vmem_spec = pl.BlockSpec(memory_space=pltpu.VMEM)
+    dma = pltpu.SemaphoreType.DMA
+    return pl.pallas_call(
+        functools.partial(mix_kernel, ny, nx),
+        out_shape=jax.ShapeDtypeStruct((groups, rows, width), jnp.bfloat16),
+        in_specs=[vmem_spec, any_spec, any_spec],
+        out_specs=vmem_spec,
+        scratch_shapes=[
+            pltpu.VMEM((2 * w_out.shape[0], cols), jnp.bfloat16),
+            pltpu.VMEM((groups, rows, 2 * w_out.shape[0]), jnp.bfloat16),
+            pltpu.VMEM((CHUNKS, groups, r, cols), jnp.float32),
+            pltpu.VMEM((CHUNKS, 2, 6, groups // 2, r, block), jnp.float32),
+            pltpu.VMEM((CHUNKS, 2, 6, r, block), jnp.float32),
+            pltpu.VMEM((2, 2, rows, block), jnp.bfloat16),
+            dma((2 * nx,)), dma((2 * nx,)), dma((3,)), dma((2,)),
+            dma((2, CHUNKS * 12)), dma((2, CHUNKS * 12)), dma((2, CHUNKS * 8)), dma((2, CHUNKS * 8)), dma((2, CHUNKS * 10)),
+        ],
+        compiler_params=pltpu.CompilerParams(collective_id=3, has_side_effects=True, vmem_limit_bytes=48 * 1024 * 1024),
+        name="mix",
+    )(o_parts, w_out, tokens.reshape(groups, rows, width))
 
 
 def solution(mesh):
@@ -50,10 +351,9 @@
             lax.dynamic_slice_in_dim(value_new, first_group, shard_groups, 1),
             lengths,
         )
-        attended = lax.all_to_all(attended.reshape(local_rows, heads_shard, head_dim), "model", 1, 0, tiled=True)
-        partial = jnp.dot(attended.reshape(batch_all, heads_local * head_dim), w_out, preferred_element_type=jnp.float32)
-        mixed_sum = lax.psum(partial, ("heads", "model"))
-        out_tokens = (tokens.astype(jnp.float32) + mixed_sum).astype(jnp.bfloat16)
+        chips = model_count // 2
+        o_parts = attended.reshape(local_rows, chips, heads_shard // chips * head_dim).transpose(1, 0, 2)
+        out_tokens = mix(heads_count, chips, o_parts, w_out, tokens).reshape(tokens.shape)
         return (out_tokens, key_new, value_new)
 
     cache_spec = P(("replica", "model"), None, None, None)

time: 191 us -> 110 us (0.58)
  waiting for transfers between devices: 111 us -> 0.01 us
  Pallas kernels: 0 us -> 62.9 us
  between operations: 14.2 us -> 0.79 us
  blocking collectives: 9.86 us -> 0 us
  other arithmetic: 8.54 us -> 0.85 us
  matrix products: 38.6 us -> 34.2 us
  local copies, waits for them, and re-layouts: 2.76 us -> 4.71 us
    psum x1 -> x0, waiting for transfers between devices: 111 us -> none  [local_step(): mixed_sum = lax.psum(partial, ('heads', 'model'))]
    pallas_call x0 -> x1, Pallas kernels: none -> 62.9 us  [mix(): pl.pallas_call(functools.partial(mix_kernel, ny, nx), out_shape=jax.Shape...]
    all_to_all x1 -> x0, blocking collectives: 9.86 us -> none  [local_step(): lax.all_to_all(attended.reshape(local_rows, heads_shard, head_dim), 'mode...]
    convert_element_type x1 -> x0, other arithmetic: 7.69 us -> none  [local_step(): out_tokens = (tokens.astype(jnp.float32) + mixed_sum).astype(jnp.bfloat16)]
    dot_general x1 -> x0, matrix products: 4.5 us -> none  [local_step(): jnp.dot(attended.reshape(batch_all, heads_local * head_dim), w_out, prefe...]
    unnamed x12 -> x11, local copies, waits for them, and re-layouts: 1.66 us -> 3.67 us
  transfers between devices with their start and end apart: 2 -> 1, of which waited for: 1 -> 0; matrix products, arithmetic and copies ran while one was open for 7% -> 12% of each run, Pallas kernels for 0% -> 0%
where the time goes in v1:
time: 110 us; the launch traced here: 109 us
  Pallas kernels  62.9 us (57%)
  matrix products  34.2 us (31%)
  starting transfers between devices  6.01 us (5%)
  local copies, waits for them, and re-layouts  4.71 us (4%)
    pallas_call x1, Pallas kernels, mix(): pl.pallas_call(functools.partial(mix_kernel, ny, nx), out_shape=jax.Shape...  62.9 us
    dot_general x1, matrix products, local_step(): jnp.dot(own_tokens, w_key, preferred_element_type=jnp.float32)  9.06 us
    dot_general x1, matrix products, attend(): jnp.einsum('bgrd,bgtd->bgrt', queries, key_rows, preferred_element_type=j...  8.18 us
    dot_general x1, matrix products, attend(): jnp.einsum('bgrt,bgtd->bgrd', weights.astype(jnp.bfloat16), value_rows, p...  7.43 us
    all_to_all x1, starting transfers between devices, local_step(): lax.all_to_all(queries.reshape(batch_all, heads_local, head_dim), 'model'...  6.01 us
    dot_general x1, matrix products, local_step(): jnp.dot(tokens, w_query, preferred_element_type=jnp.float32)  5.2 us
    dot_general x1, matrix products, local_step(): jnp.dot(own_tokens, w_value, preferred_element_type=jnp.float32)  4.1 us
    unnamed x11, local copies, waits for them, and re-layouts  3.67 us
  transfers between devices with their start and end apart: 1, of which 0 were waited for; matrix products, arithmetic and copies ran while one was open for 12% of the time, Pallas kernels for 0%

profile of v1, /device:TPU:97, one launch (start us, length us, event | category | flops | bytes accessed | tf_op | source)
XLA Modules:
  0.0 109.4 jit_solution(18399302342640447646)
XLA Ops:
  0.6 0.0 copy-start.3
  0.6 5.2 %convolution_convert_fusion = bf16[256,256]{0,1:T(8,128)(2,1)S(1)} fusion(bf16[256,8192]{1,0:T(8,128)(2,1)} %param.8, bf16[8192,256]{1,0:T(8,128)(2,1)} %param.9), kind=kOutput, calls=%fused_computation.10 | convolution fusion | flops 1073807360 | bytes 8519680 | tf_op jit(solution)/shard_map/dot_general | solution.py:338
  5.9 0.8 copy.15
  6.6 6.0 %all-to-all-start = ((bf16[256,2,128]{2,1,0:T(2,128)(2,1)}), bf16[256,2,128]{2,1,0:T(2,128)(2,1)S(1)}, u32[]{:S(2)}, u32[]{:S(2)}) async-start(bf16[256,2,128]{2,1,0:T(2,128)(2,1)} %copy.15), calls=%async_computation | async-start | bytes 262144 | tf_op jit(solution)/shard_map/all_to_all | solution.py:339
  12.6 0.0 copy-done.3
  12.6 0.1 iota_compare_fusion
  12.7 0.0 copy-start
  12.8 9.1 %fusion.10 = bf16[4,8,8,128]{3,1,2,0:T(8,128)(2,1)S(1)} fusion(bf16[8192,1024]{1,0:T(8,128)(2,1)} %param.10, bf16[256,8192]{1,0:T(8,128)(2,1)} %param.8, s32[]{:T(128)S(6)} %select_n.21), kind=kOutput, calls=%fused_computation.13 | convolution fusion | flops 536903680 | bytes 17367044 | tf_op jit(solution)/shard_map/dot_general | solution.py:341
  21.8 1.6 %copy-done = bf16[8192,1024]{1,0:T(8,128)(2,1)S(1)} copy-done((bf16[8192,1024]{1,0:T(8,128)(2,1)S(1)}, bf16[8192,1024]{1,0:T(8,128)(2,1)}, u32[]{:S(2)}) %copy-start) | copy-done | bytes 16777240
  23.4 0.0 copy-start.1
  23.4 4.1 %fusion.11 = bf16[4,8,8,128]{3,1,2,0:T(8,128)(2,1)S(1)} fusion(bf16[8192,1024]{1,0:T(8,128)(2,1)S(1)} %copy-done, bf16[256,8192]{1,0:T(8,128)(2,1)} %param.8, s32[]{:T(128)S(6)} %select_n.21), kind=kOutput, calls=%fused_computation.14 | convolution fusion | flops 536903680 | bytes 17367044 | tf_op jit(solution)/shard_map/dot_general | solution.py:343
  27.5 0.0 copy-done.1
  27.6 0.0 copy-start.2
  27.6 0.0 all-to-all-done
  27.7 0.1 copy.17
  27.8 0.2 fusion.25
  28.0 8.2 %fusion.4 = (f32[32,2,8]{2,1,0:T(2,128)S(1)}, f32[32,2,8,1024]{3,2,1,0:T(8,128)S(1)}) fusion(pred[32,1024]{1,0:T(8,128)(4,1)S(1)} %iota_compare_fusion, bf16[32,2,8,128]{3,2,1,0:T(8,128)(2,1)S(1)} %bitcast.32, bf16[32,8,1024,128]{3,2,1,0:T(8,128)(2,1)} %param.13, s32[]{:T(128)S(6)} %select_n.19), kind=kOutput, calls=%fused_computation.6 | convolution fusion | flops 135790080 | bytes 19040260 | tf_op jit(solution)/shard_map/bgrd,bgtd->bgrt/dot_general | solution.py:17
  36.2 0.0 copy-done.2
  36.3 0.7 fusion.5
  37.0 7.4 %fusion.15 = bf16[32,2,8,128]{3,2,1,0:T(8,128)(2,1)S(1)} fusion(bf16[32,8,1024,128]{3,2,1,0:T(8,128)(2,1)} %param.14, s32[]{:T(128)S(6)} %select_n.19, f32[32,2,8,1024]{3,2,1,0:T(8,128)S(1)} %get-tuple-element.6, f32[32,2,8]{2,1,0:T(2,128)S(1)} %multiply_maximum_fusion, pred[32,1024]{1,0:T(8,128)(4,1)S(1)} %iota_compare_fusion, ...), kind=kOutput, calls=%fused_computation.16 | convolution fusion | flops 136577024 | bytes 19077124 | tf_op jit(solution)/shard_map/bgrt,bgtd->bgrd/dot_general | solution.py:25
  44.4 0.1 reshape.57
  44.5 62.9 %mix.1 = bf16[8,32,8192]{2,1,0:T(8,128)(2,1)S(1)} custom-call(bf16[4,32,512]{2,1,0:T(8,128)(2,1)S(1)} %bitcast.29, bf16[256,8192]{1,0:T(8,128)(2,1)} %wo_ref.1, bf16[8,32,8192]{2,1,0:T(8,128)(2,1)} %bitcast.30), custom_call_target="tpu_custom_call" | custom-call | tf_op jit(solution)/shard_map/mix/pallas_call | solution.py:303
  107.4 2.0 %copy.28 = bf16[256,8192]{1,0:T(8,128)(2,1)} copy(bf16[256,8192]{1,0:T(8,128)(2,1)S(1)} %bitcast.28) | data formatting | bytes 8388608
  (8 shorter events, 0.2 us)
Async XLA Ops:
  0.6 12.0 %copy-start.3 = (s32[32]{0:T(128)S(1)}, s32[32]{0:T(128)}, u32[]{:S(2)}) copy-start(s32[32]{0:T(128)} %param.15) | copy-start | bytes 388
  6.6 21.0 %all-to-all-start = ((bf16[256,2,128]{2,1,0:T(2,128)(2,1)}), bf16[256,2,128]{2,1,0:T(2,128)(2,1)S(1)}, u32[]{:S(2)}, u32[]{:S(2)}) async-start(bf16[256,2,128]{2,1,0:T(2,128)(2,1)} %copy.15), calls=%async_computation | async-start | bytes 262144 | tf_op jit(solution)/shard_map/all_to_all | solution.py:339
  12.7 10.7 %copy-start = (bf16[8192,1024]{1,0:T(8,128)(2,1)S(1)}, bf16[8192,1024]{1,0:T(8,128)(2,1)}, u32[]{:S(2)}) copy-start(bf16[8192,1024]{1,0:T(8,128)(2,1)} %param.11) | copy-start | bytes 50331652
  23.4 4.1 %copy-start.1 = (bf16[4,8,8,128]{3,2,1,0:T(8,128)(2,1)}, bf16[4,8,8,128]{3,2,1,0:T(8,128)(2,1)S(1)}, u32[]{:S(2)}) copy-start(bf16[4,8,8,128]{3,2,1,0:T(8,128)(2,1)S(1)} %copy.21) | copy-start | bytes 196612
  27.6 8.6 %copy-start.2 = (bf16[4,8,8,128]{3,2,1,0:T(8,128)(2,1)}, bf16[4,8,8,128]{3,2,1,0:T(8,128)(2,1)S(1)}, u32[]{:S(2)}) copy-start(bf16[4,8,8,128]{3,2,1,0:T(8,128)(2,1)S(1)} %copy.22) | copy-start | bytes 196612

commit v2 on v1

--- a/solution.py
+++ b/solution.py
@@ -8,23 +8,11 @@
 from jax.sharding import PartitionSpec as P
 
 MESH = pl.DeviceIdType.MESH
-CHUNKS = 2
-OFFSET = 2
-
-
-def attend(queries, key_rows, value_rows, key_last, value_last, seq_len):
-    score_scale = queries.shape[-1] ** -0.5
-    scores = jnp.einsum("bgrd,bgtd->bgrt", queries, key_rows, preferred_element_type=jnp.float32) * score_scale
-    score_new = jnp.einsum("bgrd,bgd->bgr", queries, key_last, preferred_element_type=jnp.float32) * score_scale
-    positions = lax.broadcasted_iota(jnp.int32, (1, 1, 1, key_rows.shape[2]), 3)
-    scores = jnp.where(positions < seq_len[:, None, None, None], scores, -jnp.inf)
-    score_max = jnp.maximum(jnp.max(scores, axis=-1), score_new)
-    weights = jnp.exp(scores - score_max[..., None])
-    weight_new = jnp.exp(score_new - score_max)
-    denom_sum = jnp.sum(weights, axis=-1) + weight_new
-    weighted_sum = jnp.einsum("bgrt,bgtd->bgrd", weights.astype(jnp.bfloat16), value_rows, preferred_element_type=jnp.float32)
-    weighted_sum = weighted_sum + weight_new.astype(jnp.bfloat16).astype(jnp.float32)[..., None] * value_last.astype(jnp.float32)[:, :, None, :]
-    return (weighted_sum / denom_sum[..., None]).astype(jnp.bfloat16)
+CHUNKS = 1
+OFFSET = 1
+CHUNK_K = 8
+SLOTS = 8
+SEQS = 2
 
 
 def mix_kernel(ny, nx, o_ref, wo_ref, tok_ref, out_ref,
@@ -320,39 +308,197 @@
     )(o_parts, w_out, tokens.reshape(groups, rows, width))
 
 
+def front_kernel(ny, nx, tok_ref, wq_ref, wk_ref, wv_ref, kc_ref, vc_ref, len_ref,
+                 o_ref, kn_ref, vn_ref,
+                 x_buf, wq_buf, wkv_buf, acc_q, acc_kv, q_send, q_recv, q_rows, kv_send, kv_all, kv_rows, kn_rows, o_rows, k_buf, v_buf,
+                 x_sem, wq_sem, wk_sem, wv_sem, k_sem, v_sem, q_ss, q_rs, kv_ss, kv_rs):
+    y = lax.axis_index("heads")
+    model = lax.axis_index("model")
+    nm = 2 * nx
+    batch, width = x_buf.shape
+    rows = batch // nm
+    kc = width // CHUNK_K
+    head = kc_ref.shape[3]
+    context = kc_ref.shape[2]
+    groups = kc_ref.shape[1] // ny
+    kv_cols = groups * head
+    heads = nm * (wq_ref.shape[1] // head)
+    per_group = heads // groups
+    hl = wq_ref.shape[1] // head
+
+    def dev(yy, mm):
+        return {"heads": lax.rem(yy + ny, ny), "model": lax.rem(mm + nm, nm)}
+
+    barrier = pltpu.get_barrier_semaphore()
+    peers = [dev(y, model + s) for s in range(1, nm)] + [dev(y + s, model) for s in range(1, ny)]
+    for peer in peers:
+        pl.semaphore_signal(barrier, inc=1, device_id=peer, device_id_type=MESH)
+
+    copies = {}
+    my_cols = pl.ds(pl.multiple_of(y * kv_cols, kv_cols), kv_cols)
+    for i in range(CHUNK_K):
+        ks = pl.ds(i * kc, kc)
+        copies["x", i] = pltpu.make_async_copy(tok_ref.at[:, ks], x_buf.at[:, ks], x_sem.at[i])
+        copies["q", i] = pltpu.make_async_copy(wq_ref.at[ks], wq_buf.at[ks], wq_sem.at[i])
+        copies["x", i].start()
+        copies["q", i].start()
+    for i in range(CHUNK_K):
+        ks = pl.ds(i * kc, kc)
+        copies["k", i] = pltpu.make_async_copy(wk_ref.at[ks, my_cols], wkv_buf.at[ks, 0:kv_cols], wk_sem.at[i])
+        copies["v", i] = pltpu.make_async_copy(wv_ref.at[ks, my_cols], wkv_buf.at[ks, kv_cols:2 * kv_cols], wv_sem.at[i])
+        copies["k", i].start()
+        copies["v", i].start()
+
+    def cache_copies(b, slot):
+        gs = pl.ds(y * groups, groups)
+        return (pltpu.make_async_copy(kc_ref.at[b, gs], k_buf.at[slot], k_sem.at[slot]),
+                pltpu.make_async_copy(vc_ref.at[b, gs], v_buf.at[slot], v_sem.at[slot]))
+
+    for b in range(SLOTS):
+        for copy in cache_copies(b, b):
+            copy.start()
+
+    for i in range(CHUNK_K):
+        ks = pl.ds(i * kc, kc)
+        copies["x", i].wait()
+        copies["q", i].wait()
+        prod = jnp.dot(x_buf[:, ks], wq_buf[ks, :], preferred_element_type=jnp.float32)
+        acc_q[...] = prod if i == 0 else acc_q[...] + prod
+    q_send[...] = acc_q[...].astype(jnp.bfloat16).reshape(nm, rows, hl * head)
+    pl.semaphore_wait(barrier, len(peers))
+    sends = []
+    for n, s in enumerate((1, 7, 2, 6, 3, 5, 4)):
+        target = lax.rem(model + s, nm)
+        copy = pltpu.make_async_remote_copy(src_ref=q_send.at[target], dst_ref=q_recv.at[model], send_sem=q_ss.at[s],
+                                            recv_sem=q_rs.at[nm - s], device_id=dev(y, target), device_id_type=MESH)
+        copy.start()
+        sends.append(copy)
+    q_recv[pl.ds(model, 1)] = q_send[pl.ds(model, 1)]
+
+    mine = pl.ds(pl.multiple_of(model * rows, rows), rows)
+    for i in range(CHUNK_K):
+        ks = pl.ds(i * kc, kc)
+        copies["k", i].wait()
+        copies["v", i].wait()
+        prod = jnp.dot(x_buf[mine, ks], wkv_buf[ks, :], preferred_element_type=jnp.float32)
+        acc_kv[...] = prod if i == 0 else acc_kv[...] + prod
+    kv_bf = acc_kv[...].astype(jnp.bfloat16)
+    kv_send[...] = kv_bf
+    kv_all[pl.ds(y, 1)] = kv_bf[None]
+    for j in range(2 * groups):
+        kv_rows[j] = kv_bf[:, j * head:(j + 1) * head].astype(jnp.float32)
+    for s in (1, 3, 2):
+        copy = pltpu.make_async_remote_copy(src_ref=kv_send, dst_ref=kv_all.at[y], send_sem=kv_ss.at[s],
+                                            recv_sem=kv_rs.at[ny - s], device_id=dev(y + s, model), device_id_type=MESH)
+        copy.start()
+        sends.append(copy)
+
+    def arrive(dst, sem):
+        pltpu.make_async_copy(dst, dst, sem).wait()
+
+    for s in range(1, nm):
+        arrive(q_recv.at[lax.rem(model + s, nm)], q_rs.at[s])
+    for src in range(nm):
+        for j in range(hl):
+            q_rows[pl.ds(src * hl + j, rows, stride=heads), :] = q_recv[src, :, j * head:(j + 1) * head].astype(jnp.float32)
+
+    scale = head ** -0.5
+    positions = lax.broadcasted_iota(jnp.int32, (per_group, context), 1)
+
+    def step(n, carry):
+        pairs = []
+        scores = []
+        news = []
+        for u in range(SEQS):
+            b = n * SEQS + u
+            slot = lax.rem(b, SLOTS)
+            for copy in cache_copies(b, slot):
+                copy.wait()
+            length = len_ref[b]
+            for g in range(groups):
+                q = q_rows[pl.ds(pl.multiple_of(b * heads + g * per_group, per_group), per_group), :]
+                s = lax.dot_general(q.astype(jnp.bfloat16), k_buf[slot, g], (((1,), (1,)), ((), ())), preferred_element_type=jnp.float32) * scale
+                s = jnp.where(positions < length, s, -jnp.inf)
+                k_last = kv_rows[g, pl.ds(b, 1), :]
+                s_new = jnp.sum(q * k_last, axis=1, keepdims=True) * scale
+                pairs.append((b, slot, g))
+                scores.append(s)
+                news.append(s_new)
+        tops = [jnp.maximum(jnp.max(s, axis=1, keepdims=True), s_new) for s, s_new in zip(scores, news)]
+        weights = [jnp.exp(s - m) for s, m in zip(scores, tops)]
+        weight_news = [jnp.exp(s_new - m) for s_new, m in zip(news, tops)]
+        sums = [jnp.sum(e, axis=1, keepdims=True) + e_new for e, e_new in zip(weights, weight_news)]
+        for (b, slot, g), e, e_new, l in zip(pairs, weights, weight_news, sums):
+            out = jnp.dot(e.astype(jnp.bfloat16), v_buf[slot, g], preferred_element_type=jnp.float32)
+            v_last = kv_rows[groups + g, pl.ds(b, 1), :]
+            out = out + e_new.astype(jnp.bfloat16).astype(jnp.float32) * v_last
+            o_rows[pl.ds(pl.multiple_of(b * heads + g * per_group, per_group), per_group), :] = out / l
+        for u in range(SEQS):
+            b = n * SEQS + u
+
+            @pl.when(b + SLOTS < rows)
+            def _():
+                for copy in cache_copies(b + SLOTS, lax.rem(b, SLOTS)):
+                    copy.start()
+        return carry
+
+    lax.fori_loop(0, rows // SEQS, step, 0)
+    hc = heads // nx
+    for h in range(heads):
+        o_ref[h // hc, :, (h % hc) * head:(h % hc + 1) * head] = o_rows[pl.ds(h, rows, stride=heads), :].astype(jnp.bfloat16)
+
+    for s in range(1, ny):
+        arrive(kv_all.at[lax.rem(y + s, ny)], kv_rs.at[s])
+    kv_heads = ny * groups
+    for part, ref in ((0, kn_ref), (1, vn_ref)):
+        for g in range(kv_heads):
+            c0 = part * kv_cols + (g % groups) * head
+            kn_rows[part, pl.ds(g, rows, stride=kv_heads), :] = kv_all[g // groups, :, c0:c0 + head].astype(jnp.float32)
+        ref[...] = kn_rows[part].reshape(rows, kv_heads, head).astype(jnp.bfloat16)
+    for copy in sends:
+        copy.wait_send()
+
+
+def front(ny, nx, tokens, w_query, w_key, w_value, key_cache, value_cache, lengths):
+    batch, width = tokens.shape
+    rows, kv_heads, context, head = key_cache.shape
+    nm = 2 * nx
+    groups = kv_heads // ny
+    kv_cols = groups * head
+    heads = nm * w_query.shape[1] // head
+    any_spec = pl.BlockSpec(memory_space=pl.ANY)
+    vmem_spec = pl.BlockSpec(memory_space=pltpu.VMEM)
+    dma = pltpu.SemaphoreType.DMA
+    bf, f32 = jnp.bfloat16, jnp.float32
+    new_shape = jax.ShapeDtypeStruct((rows, kv_heads, head), bf)
+    return pl.pallas_call(
+        functools.partial(front_kernel, ny, nx),
+        out_shape=(jax.ShapeDtypeStruct((nx, rows, heads // nx * head), bf), new_shape, new_shape),
+        in_specs=[any_spec] * 6 + [pl.BlockSpec(memory_space=pltpu.SMEM)],
+        out_specs=(vmem_spec,) * 3,
+        scratch_shapes=[
+            pltpu.VMEM((batch, width), bf), pltpu.VMEM(w_query.shape, bf), pltpu.VMEM((width, 2 * kv_cols), bf),
+            pltpu.VMEM((batch, w_query.shape[1]), f32), pltpu.VMEM((rows, 2 * kv_cols), f32),
+            pltpu.VMEM((nm, rows, w_query.shape[1]), bf), pltpu.VMEM((nm, rows, w_query.shape[1]), bf),
+            pltpu.VMEM((rows * heads, head), f32),
+            pltpu.VMEM((rows, 2 * kv_cols), bf), pltpu.VMEM((ny, rows, 2 * kv_cols), bf), pltpu.VMEM((2 * groups, rows, head), f32),
+            pltpu.VMEM((2, rows * kv_heads, head), f32), pltpu.VMEM((rows * heads, head), f32),
+            pltpu.VMEM((SLOTS, groups, context, head), bf), pltpu.VMEM((SLOTS, groups, context, head), bf),
+            dma((CHUNK_K,)), dma((CHUNK_K,)), dma((CHUNK_K,)), dma((CHUNK_K,)), dma((SLOTS,)), dma((SLOTS,)),
+            dma((nm,)), dma((nm,)), dma((ny,)), dma((ny,)),
+        ],
+        compiler_params=pltpu.CompilerParams(collective_id=5, has_side_effects=True, vmem_limit_bytes=48 * 1024 * 1024),
+        name="front",
+    )(tokens, w_query, w_key, w_value, key_cache, value_cache, lengths)
+
+
 def solution(mesh):
     heads_count = mesh.shape["heads"]
     model_count = mesh.shape["model"]
 
     def local_step(tokens, w_query, w_key, w_value, w_out, key_cache, value_cache, lengths):
-        batch_all = tokens.shape[0]
-        local_rows = key_cache.shape[0]
-        kv_count = key_cache.shape[1]
-        head_dim = key_cache.shape[3]
-        heads_local = w_query.shape[1] // head_dim
-        heads_shard = heads_local * model_count
-        group_size = heads_shard * heads_count // kv_count
-        shard_groups = max(1, heads_shard // group_size)
-        head_index = lax.axis_index("heads")
-        model_index = lax.axis_index("model")
-        queries = jnp.dot(tokens, w_query, preferred_element_type=jnp.float32).astype(jnp.bfloat16)
-        queries = lax.all_to_all(queries.reshape(batch_all, heads_local, head_dim), "model", 0, 1, tiled=True)
-        own_tokens = lax.dynamic_slice_in_dim(tokens, model_index * local_rows, local_rows, 0)
-        key_new = jnp.dot(own_tokens, w_key, preferred_element_type=jnp.float32).astype(jnp.bfloat16)
-        key_new = key_new.reshape(local_rows, kv_count, head_dim)
-        value_new = jnp.dot(own_tokens, w_value, preferred_element_type=jnp.float32).astype(jnp.bfloat16)
-        value_new = value_new.reshape(local_rows, kv_count, head_dim)
-        first_group = head_index * heads_shard // group_size
-        attended = attend(
-            queries.reshape(local_rows, shard_groups, heads_shard // shard_groups, head_dim),
-            lax.dynamic_slice_in_dim(key_cache, first_group, shard_groups, 1),
-            lax.dynamic_slice_in_dim(value_cache, first_group, shard_groups, 1),
-            lax.dynamic_slice_in_dim(key_new, first_group, shard_groups, 1),
-            lax.dynamic_slice_in_dim(value_new, first_group, shard_groups, 1),
-            lengths,
-        )
         chips = model_count // 2
-        o_parts = attended.reshape(local_rows, chips, heads_shard // chips * head_dim).transpose(1, 0, 2)
+        o_parts, key_new, value_new = front(heads_count, chips, tokens, w_query, w_key, w_value, key_cache, value_cache, lengths)
         out_tokens = mix(heads_count, chips, o_parts, w_out, tokens).reshape(tokens.shape)
         return (out_tokens, key_new, value_new)
 

time: 110 us -> 94.3 us (0.86)
  matrix products: 34.2 us -> 0 us
  Pallas kernels: 62.9 us -> 87.4 us
  starting transfers between devices: 6.01 us -> 0 us
  local copies, waits for them, and re-layouts: 4.71 us -> 6.11 us
    dot_general x6 -> x0, matrix products: 34.2 us -> none  [the longest x1 9.06 us: local_step(): jnp.dot(own_tokens, w_key, preferred_element_type=jnp.float32)]
    pallas_call x0 -> x1, Pallas kernels: none -> 26.8 us  [front(): pl.pallas_call(functools.partial(front_kernel, ny, nx), out_shape=(jax.Sh...]
    all_to_all x1 -> x0, starting transfers between devices: 6.01 us -> none  [local_step(): lax.all_to_all(queries.reshape(batch_all, heads_local, head_dim), 'model'...]
    unnamed x11 -> x7, local copies, waits for them, and re-layouts: 3.67 us -> 6.11 us
    pallas_call x1, Pallas kernels: 62.9 us -> 60.6 us  [mix(): pl.pallas_call(functools.partial(mix_kernel, ny, nx), out_shape=jax.Shape...]
  transfers between devices with their start and end apart: 1 -> 0, of which waited for: 0 -> 0; matrix products, arithmetic and copies ran while one was open for 12% -> 0% of each run, Pallas kernels for 0% -> 0%
where the time goes in v2:
time: 94.3 us; the launch traced here: 94.2 us
  Pallas kernels  87.4 us (93%)
  local copies, waits for them, and re-layouts  6.11 us (6%)
    pallas_call x1, Pallas kernels, mix(): pl.pallas_call(functools.partial(mix_kernel, ny, nx), out_shape=jax.Shape...  60.6 us
    pallas_call x1, Pallas kernels, front(): pl.pallas_call(functools.partial(front_kernel, ny, nx), out_shape=(jax.Sh...  26.8 us
    unnamed x7, local copies, waits for them, and re-layouts  6.11 us

profile of v2, /device:TPU:97, one launch (start us, length us, event | category | flops | bytes accessed | tf_op | source)
XLA Modules:
  0.0 94.2 jit_solution(1581916861572788248)
XLA Ops:
  0.6 0.0 copy-start
  0.6 2.2 %copy-done = bf16[256,8192]{1,0:T(8,128)(2,1)S(1)} copy-done((bf16[256,8192]{1,0:T(8,128)(2,1)S(1)}, bf16[256,8192]{1,0:T(8,128)(2,1)}, u32[]{:S(2)}) %copy-start) | copy-done | bytes 4194328
  2.8 0.0 copy-start.1
  2.8 0.7 copy-done.1
  3.5 26.8 %front.1 = (bf16[4,32,512]{2,1,0:T(8,128)(2,1)S(1)}, bf16[32,8,128]{2,1,0:T(8,128)(2,1)S(1)}, bf16[32,8,128]{2,1,0:T(8,128)(2,1)S(1)}) custom-call(bf16[256,8192]{1,0:T(8,128)(2,1)S(1)} %copy-done, bf16[8192,256]{1,0:T(8,128)(2,1)} %wq_ref.1, bf16[8192,1024]{1,0:T(8,128)(2,1)} %wk_ref.1, bf16[8192,1024]{1,0:T(8,128)(2,1)} %wv_ref.1, ...), custom_call_target="tpu_custom_call" | custom-call | tf_op jit(solution)/shard_map/front/pallas_call | solution.py:474
  30.3 60.6 %mix.1 = bf16[8,32,8192]{2,1,0:T(8,128)(2,1)S(1)} custom-call(bf16[4,32,512]{2,1,0:T(8,128)(2,1)S(1)} %get-tuple-element.6.o_ref, bf16[256,8192]{1,0:T(8,128)(2,1)} %wo_ref.1, bf16[8,32,8192]{2,1,0:T(8,128)(2,1)} %bitcast.2), custom_call_target="tpu_custom_call" | custom-call | tf_op jit(solution)/shard_map/mix/pallas_call | solution.py:291
  90.9 2.0 %copy.14 = bf16[256,8192]{1,0:T(8,128)(2,1)} copy(bf16[256,8192]{1,0:T(8,128)(2,1)S(1)} %bitcast.3) | data formatting | bytes 8388608
  92.9 0.6 copy.15
  93.5 0.6 copy.16
Async XLA Ops:
  0.6 2.2 %copy-start = (bf16[256,8192]{1,0:T(8,128)(2,1)S(1)}, bf16[256,8192]{1,0:T(8,128)(2,1)}, u32[]{:S(2)}) copy-start(bf16[256,8192]{1,0:T(8,128)(2,1)} %tok_ref.1) | copy-start | bytes 12582916
  2.8 0.7 copy-start.1

commit v3 on v0

v3 whole, which is shorter than its diff:
```python
import functools

import jax
import jax.numpy as jnp
from jax import lax
from jax.experimental import pallas as pl
from jax.experimental.pallas import tpu as pltpu
from jax.sharding import PartitionSpec as P

MESH = pl.DeviceIdType.MESH
CHUNKS = 4
CHUNK_K = 8
SLOTS = 16
SEQS = 4


def layer_kernel(ny, nx, tok_ref, wq_ref, wk_ref, wv_ref, wo_ref, kc_ref, vc_ref, len_ref,
                 out_ref, kn_ref, vn_ref,
                 x_buf, wq_buf, wkv_buf, acc_q, acc_kv, q_send, q_recv, q_rows, kv_send, kv_all, kv_rows, kn_rows, o_rows, k_buf, v_buf,
                 w_buf, o_send, o_all, part, recv1, recv2,
                 x_sem, wq_sem, wk_sem, wv_sem, k_sem, v_sem, w_sem, sem_q, sem_kv, sem_o, sems1, sems2, sems3, sems4, sems_d):
    y = lax.axis_index("heads")
    model = lax.axis_index("model")
    x = lax.div(model, 2)
    core = lax.rem(model, 2)
    nm = 2 * nx
    batch, width = x_buf.shape
    rows = batch // nm
    kc = width // CHUNK_K
    head = kc_ref.shape[3]
    context = kc_ref.shape[2]
    groups = kc_ref.shape[1] // ny
    kv_cols = groups * head
    hl = wq_ref.shape[1] // head
    heads = nm * hl
    per_group = heads // groups
    depth = wo_ref.shape[0]
    cols = width // 2
    half = cols // 2
    block = half // 4
    hg = nm // 2
    r = rows // CHUNKS

    def dev(yy, xx, cc):
        return {"heads": lax.rem(yy + ny, ny), "model": 2 * lax.rem(xx + nx, nx) + cc}

    def dev_m(mm):
        return {"heads": y, "model": lax.rem(mm + nm, nm)}

    partner = dev(y, x, 1 - core)
    x_next, x_prev = dev(y, x + 1, core), dev(y, x - 1, core)
    y_next, y_prev = dev(y + 1, x, core), dev(y - 1, x, core)

    barrier = pltpu.get_barrier_semaphore()
    peers = [dev_m(model + s) for s in range(1, nm)] + [dev(y + s, x, core) for s in range(1, ny)]
    for peer in peers:
        pl.semaphore_signal(barrier, inc=1, device_id=peer, device_id_type=MESH)

    sends = []

    def remote(src, dst, send_sem, recv_sem, target):
        copy = pltpu.make_async_remote_copy(src_ref=src, dst_ref=dst, send_sem=send_sem, recv_sem=recv_sem,
                                            device_id=target, device_id_type=MESH)
        copy.start()
        sends.append(copy)

    def arrive(dst, sem):
        pltpu.make_async_copy(dst, dst, sem).wait()

    copies = {}
    kv_here = pl.ds(pl.multiple_of(y * kv_cols, kv_cols), kv_cols)
    for i in range(CHUNK_K):
        ks = pl.ds(i * kc, kc)
        copies["x", i] = pltpu.make_async_copy(tok_ref.at[:, ks], x_buf.at[:, ks], x_sem.at[i])
        copies["q", i] = pltpu.make_async_copy(wq_ref.at[ks], wq_buf.at[ks], wq_sem.at[i])
        copies["x", i].start()
        copies["q", i].start()

    def cache_copies(b, slot):
        gs = pl.ds(y * groups, groups)
        return (pltpu.make_async_copy(kc_ref.at[b, gs], k_buf.at[slot], k_sem.at[slot]),
                pltpu.make_async_copy(vc_ref.at[b, gs], v_buf.at[slot], v_sem.at[slot]))

    for i in range(CHUNK_K):
        ks = pl.ds(i * kc, kc)
        copies["x", i].wait()
        copies["q", i].wait()
        copies["k", i] = pltpu.make_async_copy(wk_ref.at[ks, kv_here], wkv_buf.at[ks, 0:kv_cols], wk_sem.at[i])
        copies["v", i] = pltpu.make_async_copy(wv_ref.at[ks, kv_here], wkv_buf.at[ks, kv_cols:2 * kv_cols], wv_sem.at[i])
        copies["k", i].start()
        copies["v", i].start()
        prod = jnp.dot(x_buf[:, ks], wq_buf[ks, :], preferred_element_type=jnp.float32)
        acc_q[...] = prod if i == 0 else acc_q[...] + prod
    q_send[...] = acc_q[...].astype(jnp.bfloat16).reshape(nm, rows, hl * head)
    pl.semaphore_wait(barrier, len(peers))
    for s in [4, 3, 5, 2, 6, 1, 7]:
        target = lax.rem(model + s, nm)
        remote(q_send.at[target], q_recv.at[model], sem_q.at[0, s], sem_q.at[1, nm - s], dev_m(target))
    q_recv[pl.ds(model, 1)] = q_send[pl.ds(model, 1)]

    mine = pl.ds(pl.multiple_of(model * rows, rows), rows)
    for i in range(CHUNK_K):
        ks = pl.ds(i * kc, kc)
        copies["k", i].wait()
        copies["v", i].wait()
        for b in range(i * SLOTS // CHUNK_K, (i + 1) * SLOTS // CHUNK_K):
            for copy in cache_copies(b, b):
                copy.start()
        prod = jnp.dot(x_buf[mine, ks], wkv_buf[ks, :], preferred_element_type=jnp.float32)
        acc_kv[...] = prod if i == 0 else acc_kv[...] + prod
    kv_bf = acc_kv[...].astype(jnp.bfloat16)
    kv_send[...] = kv_bf
    kv_all[pl.ds(y, 1)] = kv_bf[None]
    for j in range(2 * groups):
        kv_rows[j] = kv_bf[:, j * head:(j + 1) * head].astype(jnp.float32)
    for s in (2, 1, 3):
        remote(kv_send, kv_all.at[y], sem_kv.at[0, s], sem_kv.at[1, ny - s], dev(y + s, x, core))

    my_cols = pl.ds(pl.multiple_of(core * cols, cols), cols)
    other_cols = pl.ds(pl.multiple_of((1 - core) * cols, cols), cols)
    my_rows = pl.ds(pl.multiple_of(core * depth, depth), depth)
    other_rows = pl.ds(pl.multiple_of((1 - core) * depth, depth), depth)
    own_w = pltpu.make_async_copy(wo_ref.at[:, my_cols], w_buf.at[my_rows], w_sem.at[2])
    own_w.start()
    remote(wo_ref.at[:, other_cols], w_buf.at[my_rows], w_sem.at[0], w_sem.at[1], partner)

    for s in range(1, nm):
        arrive(q_recv.at[lax.rem(model + s, nm)], sem_q.at[1, s])
    for src in range(nm):
        for j in range(hl):
            q_rows[pl.ds(src * hl + j, rows, stride=heads), :] = q_recv[src, :, j * head:(j + 1) * head].astype(jnp.float32)

    scale = head ** -0.5
    hc = heads // nx

    def attend(k):
        def step(n, carry):
            positions = lax.broadcasted_iota(jnp.int32, (per_group, context), 1)
            pairs, scores, news = [], [], []
            for u in range(SEQS):
                b = k * r + n * SEQS + u
                slot = lax.rem(b, SLOTS)
                for copy in cache_copies(b, slot):
                    copy.wait()
                length = len_ref[b]
                for g in range(groups):
                    q = q_rows[pl.ds(pl.multiple_of(b * heads + g * per_group, per_group), per_group), :]
                    s = lax.dot_general(q.astype(jnp.bfloat16), k_buf[slot, g], (((1,), (1,)), ((), ())), preferred_element_type=jnp.float32) * scale
                    s = jnp.where(positions < length, s, -jnp.inf)
                    s_new = jnp.sum(q * kv_rows[g, pl.ds(b, 1), :], axis=1, keepdims=True) * scale
                    pairs.append((b, slot, g))
                    scores.append(s)
                    news.append(s_new)
            tops = [jnp.maximum(jnp.max(s, axis=1, keepdims=True), s_new) for s, s_new in zip(scores, news)]
            weights = [jnp.exp(s - m) for s, m in zip(scores, tops)]
            weight_news = [jnp.exp(s_new - m) for s_new, m in zip(news, tops)]
            sums = [jnp.sum(e, axis=1, keepdims=True) + e_new for e, e_new in zip(weights, weight_news)]
            for (b, slot, g), e, e_new, l in zip(pairs, weights, weight_news, sums):
                out = jnp.dot(e.astype(jnp.bfloat16), v_buf[slot, g], preferred_element_type=jnp.float32)
                out = out + e_new.astype(jnp.bfloat16).astype(jnp.float32) * kv_rows[groups + g, pl.ds(b, 1), :]
                o_rows[pl.ds(pl.multiple_of(b * heads + g * per_group, per_group), per_group), :] = out / l
            if (k + 1) * r + SLOTS <= rows:
                for u in range(SEQS):
                    b = k * r + n * SEQS + u
                    for copy in cache_copies(b + SLOTS, lax.rem(b, SLOTS)):
                        copy.start()
            return carry

        lax.fori_loop(0, r // SEQS, step, 0)
        for h in range(heads):
            o_send[k, h // hc, :, (h % hc) * head:(h % hc + 1) * head] = o_rows[pl.ds(k * r * heads + h, r, stride=heads), :].astype(jnp.bfloat16)
        for s in [4, 3, 5, 2, 6, 1, 7]:
            target = lax.rem(model + s, nm)
            remote(o_send.at[k, lax.div(target, 2)], o_all.at[k, model], sem_o.at[k, 0, s], sem_o.at[k, 1, nm - s], dev_m(target))
        o_all[k, pl.ds(model, 1)] = o_send[k, pl.ds(x, 1)]

    pos1 = (x, y)
    pos2 = (y, x)
    nexts = ((x_next, y_next), (y_next, x_next))
    prevs = ((x_prev, y_prev), (y_prev, x_prev))

    def cols_of(h, d):
        return pl.ds(pl.multiple_of(h * half + lax.rem(d + 4, 4) * block, block), block)

    def compute(k, h, d):
        lhs = o_all[k].reshape(nm * r, o_all.shape[3])
        acc = jnp.dot(lhs, w_buf[:, cols_of(h, d)], preferred_element_type=jnp.float32)
        part[:, k * r:(k + 1) * r, cols_of(h, d)] = acc.reshape(nm, r, block)

    low, high = pl.ds(0, hg), pl.ds(hg, hg)

    def send1(k, h, i, mi, d, target):
        kr = pl.ds(k * r, r)
        remote(part.at[mi, kr, cols_of(h, d)], recv1.at[h, i, :, kr, :], sems1.at[k, h, 0, i], sems1.at[k, h, 1, i], target)

    def wait1(k, h, i):
        arrive(recv1.at[h, i, :, pl.ds(k * r, r), :], sems1.at[k, h, 1, i])

    def s0(k):
        for s in range(1, nm):
            arrive(o_all.at[k, lax.rem(model + s, nm)], sem_o.at[k, 1, s])
        if k == 0:
            own_w.wait()
            arrive(w_buf.at[other_rows], w_sem.at[1])
        for h in range(2):
            p = pos1[h]
            compute(k, h, p + 2)
            send1(k, h, 0, low, p + 2, nexts[h][0])
            send1(k, h, 1, high, p + 2, prevs[h][0])
        for h in range(2):
            p = pos1[h]
            compute(k, h, p + 1)
            send1(k, h, 2, high, p + 1, nexts[h][0])
            compute(k, h, p - 1)
            send1(k, h, 3, low, p - 1, prevs[h][0])
        for h in range(2):
            compute(k, h, pos1[h])

    def s1(k):
        ks = slice(k * r, (k + 1) * r)
        for h in range(2):
            p = pos1[h]
            c = cols_of(h, p + 1)
            wait1(k, h, 0)
            part[0:hg, ks, c] = part[0:hg, ks, c] + recv1[h, 0, :, ks, :]
            send1(k, h, 4, low, p + 1, nexts[h][0])
            c = cols_of(h, p - 1)
            wait1(k, h, 1)
            part[hg:nm, ks, c] = part[hg:nm, ks, c] + recv1[h, 1, :, ks, :]
            send1(k, h, 5, high, p - 1, prevs[h][0])

    def send2(h, i, mi, target):
        remote(part.at[mi, :, cols_of(h, pos1[h])], recv2.at[h, i], sems2.at[h, 0, i], sems2.at[h, 1, i], target)

    def wait2(h, i):
        arrive(recv2.at[h, i], sems2.at[h, 1, i])

    def around(q):
        return lax.rem(q + 2, 4), lax.rem(q + 1, 4), lax.rem(q + 3, 4)

    def s2():
        for h in range(2):
            c = cols_of(h, pos1[h])
            far, up, down = around(pos2[h])
            for k in range(CHUNKS):
                for i in (2, 3, 4, 5):
                    wait1(k, h, i)
            part[0:hg, :, c] = part[0:hg, :, c] + recv1[h, 3] + recv1[h, 4]
            part[hg:nm, :, c] = part[hg:nm, :, c] + recv1[h, 2] + recv1[h, 5]
            send2(h, 0, 2 * far, nexts[h][1])
            send2(h, 1, 2 * far + 1, prevs[h][1])
            send2(h, 2, 2 * up + 1, nexts[h][1])
            send2(h, 3, 2 * down, prevs[h][1])

    def s3():
        for h in range(2):
            c = cols_of(h, pos1[h])
            far, up, down = around(pos2[h])
            wait2(h, 0)
            part[2 * up, :, c] = part[2 * up, :, c] + recv2[h, 0]
            send2(h, 4, 2 * up, nexts[h][1])
            wait2(h, 1)
            part[2 * down + 1, :, c] = part[2 * down + 1, :, c] + recv2[h, 1]
            send2(h, 5, 2 * down + 1, prevs[h][1])

    def region(h, j, d, sub=None, cc=None):
        c0 = pl.multiple_of((core if cc is None else cc) * cols + h * half + lax.rem(d + 4, 4) * block, block)
        j = lax.rem(j + 4, 4)
        mi = pl.ds(2 * j, 2) if sub is None else pl.ds(2 * j + sub, 1)
        return out_ref.at[mi, :, pl.ds(c0, block)]

    def push(reg, sems, index, target):
        remote(reg, reg, sems.at[(0,) + index], sems.at[(1,) + index], target)

    def pulled(reg, sems, index):
        arrive(reg, sems.at[(1,) + index])

    def spread(h, n, j):
        p = pos1[h]
        push(region(h, j, p), sems4, (h, n, 0), nexts[h][0])
        push(region(h, j, p), sems4, (h, n, 1), prevs[h][0])
        push(region(h, j, p), sems_d, (h, n, 0), partner)

    def relay(h, n, j):
        p = pos1[h]
        pulled(region(h, j, p - 1), sems4, (h, n, 0))
        push(region(h, j, p - 1, 0), sems4, (h, n, 2), nexts[h][0])
        push(region(h, j, p - 1), sems_d, (h, n, 1), partner)
        pulled(region(h, j, p + 1), sems4, (h, n, 1))
        push(region(h, j, p + 1, 1), sems4, (h, n, 3), prevs[h][0])
        push(region(h, j, p + 1), sems_d, (h, n, 2), partner)

    def finish(h, n, j):
        p = pos1[h]
        for sub in range(2):
            reg = region(h, j, p + 2, sub)
            pulled(reg, sems4, (h, n, 2 + sub))
            push(reg, sems_d, (h, n, 3 + sub), partner)

    def s4():
        for h in range(2):
            p, q = pos1[h], pos2[h]
            c = cols_of(h, p)
            for i in (2, 3, 4, 5):
                wait2(h, i)
            oc = pl.ds(pl.multiple_of(core * cols + h * half + p * block, block), block)
            for sub, plain, summed in ((0, 3, 4), (1, 2, 5)):
                mi = 2 * q + sub
                total = part[mi, :, c] + recv2[h, plain] + recv2[h, summed]
                total = x_buf[pl.ds(pl.multiple_of(mi * rows, rows), rows), oc].astype(jnp.float32) + total
                out_ref[mi, :, oc] = total.astype(out_ref.dtype)
            push(region(h, q, p), sems3, (h, 0), nexts[h][1])
            push(region(h, q, p), sems3, (h, 1), prevs[h][1])
        for h in range(2):
            spread(h, 0, pos2[h])

    def s5():
        for h in range(2):
            p, q = pos1[h], pos2[h]
            pulled(region(h, q - 1, p), sems3, (h, 0))
            push(region(h, q - 1, p, 0), sems3, (h, 2), nexts[h][1])
            pulled(region(h, q + 1, p), sems3, (h, 1))
            push(region(h, q + 1, p, 1), sems3, (h, 3), prevs[h][1])
        for h in range(2):
            spread(h, 1, pos2[h] - 1)
            spread(h, 2, pos2[h] + 1)

    def s6():
        for h in range(2):
            relay(h, 0, pos2[h])
        for h in range(2):
            p, q = pos1[h], pos2[h]
            pulled(region(h, q + 2, p, 0), sems3, (h, 2))
            pulled(region(h, q + 2, p, 1), sems3, (h, 3))
            spread(h, 3, q + 2)

    def s7():
        for h in range(2):
            relay(h, 1, pos2[h] - 1)
            relay(h, 2, pos2[h] + 1)
        for h in range(2):
            finish(h, 0, pos2[h])
        for h in range(2):
            relay(h, 3, pos2[h] + 2)
        for n, d in ((1, -1), (2, 1), (3, 2)):
            for h in range(2):
                finish(h, n, pos2[h] + d)

    def new_rows():
        for s in range(1, ny):
            arrive(kv_all.at[lax.rem(y + s, ny)], sem_kv.at[1, s])
        kv_heads = ny * groups
        for half_, ref in ((0, kn_ref), (1, vn_ref)):
            for g in range(kv_heads):
                c0 = half_ * kv_cols + (g % groups) * head
                kn_rows[half_, pl.ds(g, rows, stride=kv_heads), :] = kv_all[g // groups, :, c0:c0 + head].astype(jnp.float32)
            ref[...] = kn_rows[half_].reshape(rows, kv_heads, head).astype(jnp.bfloat16)

    attend(0)
    attend(1)
    s0(0)
    attend(2)
    s1(0)
    s0(1)
    attend(3)
    s1(1)
    s0(2)
    new_rows()
    s1(2)
    s0(3)
    s1(3)
    s2()
    s3()
    s4()
    s5()
    s6()
    s7()
    for h in range(2):
        p, q = pos1[h], pos2[h]
        for n, d in ((0, 0), (1, -1), (2, 1), (3, 2)):
            for i, (dp, sub) in enumerate(((0, None), (-1, None), (1, None), (2, 0), (2, 1))):
                pulled(region(h, q + d, p + dp, sub, 1 - core), sems_d, (h, n, i))
    for copy in sends:
        copy.wait_send()


def layer(ny, nx, tokens, w_query, w_key, w_value, w_out, key_cache, value_cache, lengths):
    batch, width = tokens.shape
    rows, kv_heads, context, head = key_cache.shape
    nm = 2 * nx
    groups = kv_heads // ny
    kv_cols = groups * head
    heads = nm * w_query.shape[1] // head
    depth = w_out.shape[0]
    block = width // 16
    r = rows // CHUNKS
    hbm_spec = pl.BlockSpec(memory_space=pltpu.HBM)
    vmem_spec = pl.BlockSpec(memory_space=pltpu.VMEM)
    dma = pltpu.SemaphoreType.DMA
    bf, f32 = jnp.bfloat16, jnp.float32
    new_shape = jax.ShapeDtypeStruct((rows, kv_heads, head), bf)
    return pl.pallas_call(
        functools.partial(layer_kernel, ny, nx),
        out_shape=(jax.ShapeDtypeStruct((nm, rows, width), bf), new_shape, new_shape),
        in_specs=[hbm_spec] * 7 + [pl.BlockSpec(memory_space=pltpu.SMEM)],
        out_specs=(vmem_spec,) * 3,
        scratch_shapes=[
            pltpu.VMEM((batch, width), bf), pltpu.VMEM(w_query.shape, bf), pltpu.VMEM((width, 2 * kv_cols), bf),
            pltpu.VMEM((batch, w_query.shape[1]), f32), pltpu.VMEM((rows, 2 * kv_cols), f32),
            pltpu.VMEM((nm, rows, w_query.shape[1]), bf), pltpu.VMEM((nm, rows, w_query.shape[1]), bf),
            pltpu.VMEM((rows * heads, head), f32),
            pltpu.VMEM((rows, 2 * kv_cols), bf), pltpu.VMEM((ny, rows, 2 * kv_cols), bf), pltpu.VMEM((2 * groups, rows, head), f32),
            pltpu.VMEM((2, rows * kv_heads, head), f32), pltpu.VMEM((rows * heads, head), f32),
            pltpu.VMEM((SLOTS, groups, context, head), bf), pltpu.VMEM((SLOTS, groups, context, head), bf),
            pltpu.VMEM((2 * depth, width // 2), bf),
            pltpu.VMEM((CHUNKS, nx, r, 2 * depth), bf), pltpu.VMEM((CHUNKS, nm, r, 2 * depth), bf),
            pltpu.VMEM((nm, rows, width // 2), f32),
            pltpu.VMEM((2, 6, nm // 2, rows, block), f32),
            pltpu.VMEM((2, 6, rows, block), f32),
            dma((CHUNK_K,)), dma((CHUNK_K,)), dma((CHUNK_K,)), dma((CHUNK_K,)), dma((SLOTS,)), dma((SLOTS,)), dma((3,)),
            dma((2, nm)), dma((2, ny)), dma((CHUNKS, 2, nm)), dma((CHUNKS, 2, 2, 6)), dma((2, 2, 6)), dma((2, 2, 4)),
            dma((2, 2, 4, 4)), dma((2, 2, 4, 5)),
        ],
        compiler_params=pltpu.CompilerParams(collective_id=5, has_side_effects=True, vmem_limit_bytes=47 * 1024 * 1024),
        name="layer",
    )(tokens, w_query, w_key, w_value, w_out, key_cache, value_cache, lengths)


def solution(mesh):
    heads_count = mesh.shape["heads"]
    chips = mesh.shape["model"] // 2

    def local_step(tokens, w_query, w_key, w_value, w_out, key_cache, value_cache, lengths):
        out, key_new, value_new = layer(heads_count, chips, tokens, w_query, w_key, w_value, w_out, key_cache, value_cache, lengths)
        return (out.reshape(tokens.shape), key_new, value_new)

    cache_spec = P(("replica", "model"), None, None, None)
    new_spec = P(("replica", "model"), None, None)
    return jax.shard_map(
        local_step,
        mesh=mesh,
        in_specs=(P("replica", None), P(None, ("heads", "model")), P(None, None), P(None, None), P(("heads", "model"), None), cache_spec, cache_spec, P(("replica", "model"))),
        out_specs=(P("replica", None), new_spec, new_spec),
        check_vma=False,
    )
```

time: 191 us -> 78.9 us (0.41)
  waiting for transfers between devices: 111 us -> 0 us
  Pallas kernels: 0 us -> 74.2 us
  matrix products: 38.6 us -> 0 us
  between operations: 14.2 us -> 0.65 us
  blocking collectives: 9.86 us -> 0 us
  other arithmetic: 8.54 us -> 0 us
  starting transfers between devices: 6.02 us -> 0 us
    psum x1 -> x0, waiting for transfers between devices: 111 us -> none  [local_step(): mixed_sum = lax.psum(partial, ('heads', 'model'))]
    pallas_call x0 -> x1, Pallas kernels: none -> 74.2 us  [layer(): pl.pallas_call(functools.partial(layer_kernel, ny, nx), out_shape=(jax.Sh...]
    dot_general x7 -> x0, matrix products: 38.6 us -> none  [the longest x1 9.06 us: local_step(): jnp.dot(own_tokens, w_key, preferred_element_type=jnp.float32)]
    all_to_all x1 -> x0, blocking collectives: 9.86 us -> none  [local_step(): lax.all_to_all(attended.reshape(local_rows, heads_shard, head_dim), 'mode...]
    convert_element_type x3 -> x0, other arithmetic: 7.75 us -> none  [the longest x1 7.69 us: local_step(): out_tokens = (tokens.astype(jnp.float32) + mixed_sum).astype(jnp.bfloat16)]
    all_to_all x1 -> x0, starting transfers between devices: 6.01 us -> none  [local_step(): lax.all_to_all(queries.reshape(batch_all, heads_local, head_dim), 'model'...]
    unnamed x12 -> x5, local copies, waits for them, and re-layouts: 1.66 us -> 3.92 us
  transfers between devices with their start and end apart: 2 -> 0, of which waited for: 1 -> 0; matrix products, arithmetic and copies ran while one was open for 7% -> 0% of each run, Pallas kernels for 0% -> 0%
where the time goes in v3:
time: 78.9 us; the launch traced here: 78.8 us
  Pallas kernels  74.2 us (94%)
  local copies, waits for them, and re-layouts  3.92 us (5%)
    pallas_call x1, Pallas kernels, layer(): pl.pallas_call(functools.partial(layer_kernel, ny, nx), out_shape=(jax.Sh...  74.2 us
    unnamed x5, local copies, waits for them, and re-layouts  3.92 us

profile of v3, /device:TPU:97, one launch (start us, length us, event | category | flops | bytes accessed | tf_op | source)
XLA Modules:
  0.0 78.8 jit_solution(4571886816737011291)
XLA Ops:
  0.6 0.0 copy-start
  0.6 0.6 copy-done
  1.3 74.2 %layer.1 = (bf16[8,32,8192]{2,1,0:T(8,128)(2,1)S(1)}, bf16[32,8,128]{2,1,0:T(8,128)(2,1)S(1)}, bf16[32,8,128]{2,1,0:T(8,128)(2,1)S(1)}) custom-call(bf16[256,8192]{1,0:T(8,128)(2,1)} %tok_ref.1, bf16[8192,256]{1,0:T(8,128)(2,1)} %wq_ref.1, bf16[8192,1024]{1,0:T(8,128)(2,1)} %wk_ref.1, bf16[8192,1024]{1,0:T(8,128)(2,1)} %wv_ref.1, bf16[256,8192]{1,0:T(8,128)(2,1)} %wo_ref.1, ...), custom_call_target="tpu_custom_call" | custom-call | tf_op jit(solution)/shard_map/layer/pallas_call | solution.py:402
  75.5 2.0 %copy.14 = bf16[256,8192]{1,0:T(8,128)(2,1)} copy(bf16[256,8192]{1,0:T(8,128)(2,1)S(1)} %bitcast.1) | data formatting | bytes 8388608
  77.5 0.6 copy.15
  78.1 0.6 copy.16
Async XLA Ops:
  0.6 0.7 copy-start

commit v4 on v3

--- a/solution.py
+++ b/solution.py
@@ -12,13 +12,15 @@
 CHUNK_K = 8
 SLOTS = 16
 SEQS = 4
+AHEAD = 6
 
 
 def layer_kernel(ny, nx, tok_ref, wq_ref, wk_ref, wv_ref, wo_ref, kc_ref, vc_ref, len_ref,
                  out_ref, kn_ref, vn_ref,
                  x_buf, wq_buf, wkv_buf, acc_q, acc_kv, q_send, q_recv, q_rows, kv_send, kv_all, kv_rows, kn_rows, o_rows, k_buf, v_buf,
-                 w_buf, o_send, o_all, part, recv1, recv2,
-                 x_sem, wq_sem, wk_sem, wv_sem, k_sem, v_sem, w_sem, sem_q, sem_kv, sem_o, sems1, sems2, sems3, sems4, sems_d):
+                 w_all, w_pass, o_row, o_col, part, recv2,
+                 x_sem, wq_sem, wk_sem, wv_sem, k_sem, v_sem, own_sem, sem_pair, sem_w, sem_r, sem_q, sem_kv, sem_row, sem_col, sem_pass,
+                 sems2, sems3, sems4, sems_d):
     y = lax.axis_index("heads")
     model = lax.axis_index("model")
     x = lax.div(model, 2)
@@ -38,7 +40,7 @@
     cols = width // 2
     half = cols // 2
     block = half // 4
-    hg = nm // 2
+    near = depth // 2
     r = rows // CHUNKS
 
     def dev(yy, xx, cc):
@@ -53,6 +55,7 @@
 
     barrier = pltpu.get_barrier_semaphore()
     peers = [dev_m(model + s) for s in range(1, nm)] + [dev(y + s, x, core) for s in range(1, ny)]
+    peers += [dev(y + 1, x, 1 - core), dev(y - 1, x, 1 - core)]
     for peer in peers:
         pl.semaphore_signal(barrier, inc=1, device_id=peer, device_id_type=MESH)
 
@@ -66,6 +69,59 @@
 
     def arrive(dst, sem):
         pltpu.make_async_copy(dst, dst, sem).wait()
+
+    pos1 = (x, y)
+    pos2 = (y, x)
+    nexts = ((x_next, y_next), (y_next, x_next))
+    prevs = ((x_prev, y_prev), (y_prev, x_prev))
+    halves = (pl.ds(0, near), pl.ds(near, near))
+
+    def along(h, d, cc):
+        return dev(y, x + d, cc) if h == 0 else dev(y + d, x, cc)
+
+    def block_of(h, d, cc):
+        return pl.ds(pl.multiple_of(cc * cols + h * half + lax.rem(d + 4, 4) * block, block), block)
+
+    def slot_of(h, d, cc):
+        return 2 * lax.rem(pos1[h] + d + 4, 4) + cc
+
+    def far_start(cc):
+        for h in range(2):
+            for way, target in ((0, nexts[h][0]), (1, prevs[h][0])):
+                remote(wo_ref.at[halves[way], block_of(h, pos1[h] + 2, cc)], w_pass.at[h, way, cc],
+                       sem_r.at[0, h, way, cc], sem_r.at[1, h, way, cc], target)
+
+    def near_start(cc, n):
+        for h in range(2):
+            for way, d in ((0, 1), (1, -1)):
+                remote(wo_ref.at[halves[n], block_of(h, pos1[h] + d, cc)], w_all.at[h, slot_of(h, 0, core), halves[n]],
+                       sem_w.at[0, h, way, cc, n], sem_w.at[1, h, way, core, n], along(h, d, cc))
+
+    def far_pass(cc):
+        for h in range(2):
+            for way, d in ((0, 1), (1, -1)):
+                arrive(w_pass.at[h, way, cc], sem_r.at[1, h, way, cc])
+                remote(w_pass.at[h, way, cc], w_all.at[h, slot_of(h, -d, core), halves[way]],
+                       sem_w.at[0, h, way, cc, 2], sem_w.at[1, h, way, core, 2], along(h, d, cc))
+
+    own_copies = []
+
+    def own_start():
+        for h in range(2):
+            copy = pltpu.make_async_copy(wo_ref.at[:, block_of(h, pos1[h], core)], w_all.at[h, slot_of(h, 0, core)], own_sem.at[h])
+            copy.start()
+            own_copies.append(copy)
+            remote(wo_ref.at[:, block_of(h, pos1[h], 1 - core)], w_all.at[h, slot_of(h, 0, core)], sem_pair.at[0, h], sem_pair.at[1, h], partner)
+
+    def weights_here():
+        for h in range(2):
+            own_copies[h].wait()
+            arrive(w_all.at[h, slot_of(h, 0, 1 - core)], sem_pair.at[1, h])
+            for way, d in ((0, -1), (1, 1)):
+                for cc in range(2):
+                    for n in range(2):
+                        arrive(w_all.at[h, slot_of(h, d, cc), halves[n]], sem_w.at[1, h, way, cc, n])
+                    arrive(w_all.at[h, slot_of(h, 2, cc), halves[way]], sem_w.at[1, h, way, cc, 2])
 
     copies = {}
     kv_here = pl.ds(pl.multiple_of(y * kv_cols, kv_cols), kv_cols)
@@ -73,39 +129,47 @@
         ks = pl.ds(i * kc, kc)
         copies["x", i] = pltpu.make_async_copy(tok_ref.at[:, ks], x_buf.at[:, ks], x_sem.at[i])
         copies["q", i] = pltpu.make_async_copy(wq_ref.at[ks], wq_buf.at[ks], wq_sem.at[i])
-        copies["x", i].start()
-        copies["q", i].start()
+        copies["k", i] = pltpu.make_async_copy(wk_ref.at[ks, kv_here], wkv_buf.at[ks, 0:kv_cols], wk_sem.at[i])
+        copies["v", i] = pltpu.make_async_copy(wv_ref.at[ks, kv_here], wkv_buf.at[ks, kv_cols:2 * kv_cols], wv_sem.at[i])
 
     def cache_copies(b, slot):
         gs = pl.ds(y * groups, groups)
         return (pltpu.make_async_copy(kc_ref.at[b, gs], k_buf.at[slot], k_sem.at[slot]),
                 pltpu.make_async_copy(vc_ref.at[b, gs], v_buf.at[slot], v_sem.at[slot]))
 
+    reads = [(copies["x", i], copies["q", i]) for i in range(CHUNK_K)] + [(copies["k", i], copies["v", i]) for i in range(CHUNK_K)]
+    reads += [cache_copies(b, b) for b in range(SLOTS)]
+
+    def read_next(n):
+        for pair in reads[:n]:
+            for copy in pair:
+                copy.start()
+        del reads[:n]
+
+    read_next(AHEAD)
+    pl.semaphore_wait(barrier, len(peers))
+    far_start(0)
     for i in range(CHUNK_K):
         ks = pl.ds(i * kc, kc)
         copies["x", i].wait()
         copies["q", i].wait()
-        copies["k", i] = pltpu.make_async_copy(wk_ref.at[ks, kv_here], wkv_buf.at[ks, 0:kv_cols], wk_sem.at[i])
-        copies["v", i] = pltpu.make_async_copy(wv_ref.at[ks, kv_here], wkv_buf.at[ks, kv_cols:2 * kv_cols], wv_sem.at[i])
-        copies["k", i].start()
-        copies["v", i].start()
+        read_next(1)
         prod = jnp.dot(x_buf[:, ks], wq_buf[ks, :], preferred_element_type=jnp.float32)
         acc_q[...] = prod if i == 0 else acc_q[...] + prod
     q_send[...] = acc_q[...].astype(jnp.bfloat16).reshape(nm, rows, hl * head)
-    pl.semaphore_wait(barrier, len(peers))
     for s in [4, 3, 5, 2, 6, 1, 7]:
         target = lax.rem(model + s, nm)
         remote(q_send.at[target], q_recv.at[model], sem_q.at[0, s], sem_q.at[1, nm - s], dev_m(target))
     q_recv[pl.ds(model, 1)] = q_send[pl.ds(model, 1)]
+    far_start(1)
+    near_start(0, 0)
 
     mine = pl.ds(pl.multiple_of(model * rows, rows), rows)
     for i in range(CHUNK_K):
         ks = pl.ds(i * kc, kc)
         copies["k", i].wait()
         copies["v", i].wait()
-        for b in range(i * SLOTS // CHUNK_K, (i + 1) * SLOTS // CHUNK_K):
-            for copy in cache_copies(b, b):
-                copy.start()
+        read_next(1)
         prod = jnp.dot(x_buf[mine, ks], wkv_buf[ks, :], preferred_element_type=jnp.float32)
         acc_kv[...] = prod if i == 0 else acc_kv[...] + prod
     kv_bf = acc_kv[...].astype(jnp.bfloat16)
@@ -116,14 +180,9 @@
     for s in (2, 1, 3):
         remote(kv_send, kv_all.at[y], sem_kv.at[0, s], sem_kv.at[1, ny - s], dev(y + s, x, core))
 
-    my_cols = pl.ds(pl.multiple_of(core * cols, cols), cols)
-    other_cols = pl.ds(pl.multiple_of((1 - core) * cols, cols), cols)
-    my_rows = pl.ds(pl.multiple_of(core * depth, depth), depth)
-    other_rows = pl.ds(pl.multiple_of((1 - core) * depth, depth), depth)
-    own_w = pltpu.make_async_copy(wo_ref.at[:, my_cols], w_buf.at[my_rows], w_sem.at[2])
-    own_w.start()
-    remote(wo_ref.at[:, other_cols], w_buf.at[my_rows], w_sem.at[0], w_sem.at[1], partner)
-
+    near_start(0, 1)
+    own_start()
+    read_next(len(reads))
     for s in range(1, nm):
         arrive(q_recv.at[lax.rem(model + s, nm)], sem_q.at[1, s])
     for src in range(nm):
@@ -168,100 +227,73 @@
 
         lax.fori_loop(0, r // SEQS, step, 0)
         for h in range(heads):
-            o_send[k, h // hc, :, (h % hc) * head:(h % hc + 1) * head] = o_rows[pl.ds(k * r * heads + h, r, stride=heads), :].astype(jnp.bfloat16)
-        for s in [4, 3, 5, 2, 6, 1, 7]:
-            target = lax.rem(model + s, nm)
-            remote(o_send.at[k, lax.div(target, 2)], o_all.at[k, model], sem_o.at[k, 0, s], sem_o.at[k, 1, nm - s], dev_m(target))
-        o_all[k, pl.ds(model, 1)] = o_send[k, pl.ds(x, 1)]
-
-    pos1 = (x, y)
-    pos2 = (y, x)
-    nexts = ((x_next, y_next), (y_next, x_next))
-    prevs = ((x_prev, y_prev), (y_prev, x_prev))
-
-    def cols_of(h, d):
-        return pl.ds(pl.multiple_of(h * half + lax.rem(d + 4, 4) * block, block), block)
-
-    def compute(k, h, d):
-        lhs = o_all[k].reshape(nm * r, o_all.shape[3])
-        acc = jnp.dot(lhs, w_buf[:, cols_of(h, d)], preferred_element_type=jnp.float32)
-        part[:, k * r:(k + 1) * r, cols_of(h, d)] = acc.reshape(nm, r, block)
-
-    low, high = pl.ds(0, hg), pl.ds(hg, hg)
-
-    def send1(k, h, i, mi, d, target):
-        kr = pl.ds(k * r, r)
-        remote(part.at[mi, kr, cols_of(h, d)], recv1.at[h, i, :, kr, :], sems1.at[k, h, 0, i], sems1.at[k, h, 1, i], target)
-
-    def wait1(k, h, i):
-        arrive(recv1.at[h, i, :, pl.ds(k * r, r), :], sems1.at[k, h, 1, i])
-
-    def s0(k):
-        for s in range(1, nm):
-            arrive(o_all.at[k, lax.rem(model + s, nm)], sem_o.at[k, 1, s])
-        if k == 0:
-            own_w.wait()
-            arrive(w_buf.at[other_rows], w_sem.at[1])
-        for h in range(2):
-            p = pos1[h]
-            compute(k, h, p + 2)
-            send1(k, h, 0, low, p + 2, nexts[h][0])
-            send1(k, h, 1, high, p + 2, prevs[h][0])
-        for h in range(2):
-            p = pos1[h]
-            compute(k, h, p + 1)
-            send1(k, h, 2, high, p + 1, nexts[h][0])
-            compute(k, h, p - 1)
-            send1(k, h, 3, low, p - 1, prevs[h][0])
-        for h in range(2):
-            compute(k, h, pos1[h])
-
-    def s1(k):
+            o_row[k, core, x, h // hc, :, (h % hc) * head:(h % hc + 1) * head] = o_rows[pl.ds(k * r * heads + h, r, stride=heads), :].astype(jnp.bfloat16)
+        own = o_row.at[k, core, x]
+        for d in (2, 1, 3):
+            remote(own, own, sem_row.at[0, k, d], sem_row.at[1, k, nx - d], dev(y, x + d, core))
+        remote(own, own, sem_pass.at[0, k, 0], sem_pass.at[1, k, 0], partner)
+
+    def columns(k):
+        for d in range(1, nx):
+            got = o_row.at[k, core, lax.rem(x + d, nx)]
+            arrive(got, sem_row.at[1, k, d])
+            remote(got, got, sem_pass.at[0, k, d], sem_pass.at[1, k, d], partner)
+        for d in (2, 1, 3):
+            remote(o_row.at[k, core, :, x], o_col.at[k, y, core], sem_col.at[0, k, d], sem_col.at[1, k, ny - d], dev(y + d, x, core))
+
+    def across(k):
+        for d in range(1, ny):
+            got = o_col.at[k, lax.rem(y + d, ny), core]
+            arrive(got, sem_col.at[1, k, d])
+            remote(got, got, sem_pass.at[0, k, 3 + d], sem_pass.at[1, k, 3 + d], partner)
+
+    def project(k):
+        for d in range(nx):
+            arrive(o_row.at[k, 1 - core, lax.rem(x + d, nx)], sem_pass.at[1, k, d])
+        for d in range(1, ny):
+            arrive(o_col.at[k, lax.rem(y + d, ny), 1 - core], sem_pass.at[1, k, 3 + d])
         ks = slice(k * r, (k + 1) * r)
-        for h in range(2):
-            p = pos1[h]
-            c = cols_of(h, p + 1)
-            wait1(k, h, 0)
-            part[0:hg, ks, c] = part[0:hg, ks, c] + recv1[h, 0, :, ks, :]
-            send1(k, h, 4, low, p + 1, nexts[h][0])
-            c = cols_of(h, p - 1)
-            wait1(k, h, 1)
-            part[hg:nm, ks, c] = part[hg:nm, ks, c] + recv1[h, 1, :, ks, :]
-            send1(k, h, 5, high, p - 1, prevs[h][0])
-
-    def send2(h, i, mi, target):
-        remote(part.at[mi, :, cols_of(h, pos1[h])], recv2.at[h, i], sems2.at[h, 0, i], sems2.at[h, 1, i], target)
+        hw = o_row.shape[5]
+        acc = jnp.zeros((nm * r, block), jnp.float32)
+        for b in range(nx):
+            lhs = o_row[k, :, :, b].reshape(nm * r, hw)
+            acc = acc + jnp.dot(lhs, w_all[0, 2 * b:2 * b + 2].reshape(hw, block), preferred_element_type=jnp.float32)
+        part[0, :, :, ks, :] = acc.reshape(2, nx, r, block)
+        acc = jnp.zeros((nm * r, block), jnp.float32)
+        for d in range(ny):
+            yy = lax.rem(y + d, ny)
+            lhs = o_row[k, :, :, x] if d == 0 else o_col[k, yy]
+            acc = acc + jnp.dot(lhs.reshape(nm * r, hw), w_all[1, pl.ds(2 * yy, 2)].reshape(hw, block), preferred_element_type=jnp.float32)
+        part[1, :, :, ks, :] = acc.reshape(2, nx, r, block)
+
+    def send2(h, i, sub, q, target):
+        remote(part.at[h, sub, q], recv2.at[h, i], sems2.at[0, h, i], sems2.at[1, h, i], target)
 
     def wait2(h, i):
-        arrive(recv2.at[h, i], sems2.at[h, 1, i])
+        arrive(recv2.at[h, i], sems2.at[1, h, i])
 
     def around(q):
         return lax.rem(q + 2, 4), lax.rem(q + 1, 4), lax.rem(q + 3, 4)
 
     def s2():
         for h in range(2):
-            c = cols_of(h, pos1[h])
             far, up, down = around(pos2[h])
-            for k in range(CHUNKS):
-                for i in (2, 3, 4, 5):
-                    wait1(k, h, i)
-            part[0:hg, :, c] = part[0:hg, :, c] + recv1[h, 3] + recv1[h, 4]
-            part[hg:nm, :, c] = part[hg:nm, :, c] + recv1[h, 2] + recv1[h, 5]
-            send2(h, 0, 2 * far, nexts[h][1])
-            send2(h, 1, 2 * far + 1, prevs[h][1])
-            send2(h, 2, 2 * up + 1, nexts[h][1])
-            send2(h, 3, 2 * down, prevs[h][1])
+            send2(h, 0, 0, far, nexts[h][1])
+            send2(h, 1, 1, far, prevs[h][1])
+        for h in range(2):
+            far, up, down = around(pos2[h])
+            send2(h, 2, 1, up, nexts[h][1])
+            send2(h, 3, 0, down, prevs[h][1])
 
     def s3():
         for h in range(2):
-            c = cols_of(h, pos1[h])
             far, up, down = around(pos2[h])
             wait2(h, 0)
-            part[2 * up, :, c] = part[2 * up, :, c] + recv2[h, 0]
-            send2(h, 4, 2 * up, nexts[h][1])
+            part[h, 0, up] = part[h, 0, up] + recv2[h, 0]
+            send2(h, 4, 0, up, nexts[h][1])
             wait2(h, 1)
-            part[2 * down + 1, :, c] = part[2 * down + 1, :, c] + recv2[h, 1]
-            send2(h, 5, 2 * down + 1, prevs[h][1])
+            part[h, 1, down] = part[h, 1, down] + recv2[h, 1]
+            send2(h, 5, 1, down, prevs[h][1])
 
     def region(h, j, d, sub=None, cc=None):
         c0 = pl.multiple_of((core if cc is None else cc) * cols + h * half + lax.rem(d + 4, 4) * block, block)
@@ -300,13 +332,12 @@
     def s4():
         for h in range(2):
             p, q = pos1[h], pos2[h]
-            c = cols_of(h, p)
             for i in (2, 3, 4, 5):
                 wait2(h, i)
             oc = pl.ds(pl.multiple_of(core * cols + h * half + p * block, block), block)
             for sub, plain, summed in ((0, 3, 4), (1, 2, 5)):
                 mi = 2 * q + sub
-                total = part[mi, :, c] + recv2[h, plain] + recv2[h, summed]
+                total = part[h, sub, q] + recv2[h, plain] + recv2[h, summed]
                 total = x_buf[pl.ds(pl.multiple_of(mi * rows, rows), rows), oc].astype(jnp.float32) + total
                 out_ref[mi, :, oc] = total.astype(out_ref.dtype)
             push(region(h, q, p), sems3, (h, 0), nexts[h][1])
@@ -356,19 +387,28 @@
                 kn_rows[half_, pl.ds(g, rows, stride=kv_heads), :] = kv_all[g // groups, :, c0:c0 + head].astype(jnp.float32)
             ref[...] = kn_rows[half_].reshape(rows, kv_heads, head).astype(jnp.bfloat16)
 
+    near_start(1, 0)
     attend(0)
+    far_pass(0)
     attend(1)
-    s0(0)
+    columns(0)
+    far_pass(1)
+    near_start(1, 1)
     attend(2)
-    s1(0)
-    s0(1)
+    across(0)
+    columns(1)
+    new_rows()
     attend(3)
-    s1(1)
-    s0(2)
-    new_rows()
-    s1(2)
-    s0(3)
-    s1(3)
+    across(1)
+    columns(2)
+    columns(3)
+    weights_here()
+    project(0)
+    project(1)
+    across(2)
+    across(3)
+    project(2)
+    project(3)
     s2()
     s3()
     s4()
@@ -412,13 +452,13 @@
             pltpu.VMEM((rows, 2 * kv_cols), bf), pltpu.VMEM((ny, rows, 2 * kv_cols), bf), pltpu.VMEM((2 * groups, rows, head), f32),
             pltpu.VMEM((2, rows * kv_heads, head), f32), pltpu.VMEM((rows * heads, head), f32),
             pltpu.VMEM((SLOTS, groups, context, head), bf), pltpu.VMEM((SLOTS, groups, context, head), bf),
-            pltpu.VMEM((2 * depth, width // 2), bf),
-            pltpu.VMEM((CHUNKS, nx, r, 2 * depth), bf), pltpu.VMEM((CHUNKS, nm, r, 2 * depth), bf),
-            pltpu.VMEM((nm, rows, width // 2), f32),
-            pltpu.VMEM((2, 6, nm // 2, rows, block), f32),
+            pltpu.VMEM((2, nm, depth, block), bf), pltpu.VMEM((2, 2, 2, depth // 2, block), bf),
+            pltpu.VMEM((CHUNKS, 2, nx, nx, r, 2 * depth), bf), pltpu.VMEM((CHUNKS, ny, 2, nx, r, 2 * depth), bf),
+            pltpu.VMEM((2, 2, nx, rows, block), f32),
             pltpu.VMEM((2, 6, rows, block), f32),
-            dma((CHUNK_K,)), dma((CHUNK_K,)), dma((CHUNK_K,)), dma((CHUNK_K,)), dma((SLOTS,)), dma((SLOTS,)), dma((3,)),
-            dma((2, nm)), dma((2, ny)), dma((CHUNKS, 2, nm)), dma((CHUNKS, 2, 2, 6)), dma((2, 2, 6)), dma((2, 2, 4)),
+            dma((CHUNK_K,)), dma((CHUNK_K,)), dma((CHUNK_K,)), dma((CHUNK_K,)), dma((SLOTS,)), dma((SLOTS,)),
+            dma((2,)), dma((2, 2)), dma((2, 2, 2, 2, 3)), dma((2, 2, 2, 2)), dma((2, nm)), dma((2, ny)),
+            dma((2, CHUNKS, nx)), dma((2, CHUNKS, ny)), dma((2, CHUNKS, 7)), dma((2, 2, 6)), dma((2, 2, 4)),
             dma((2, 2, 4, 4)), dma((2, 2, 4, 5)),
         ],
         compiler_params=pltpu.CompilerParams(collective_id=5, has_side_effects=True, vmem_limit_bytes=47 * 1024 * 1024),

time: 78.9 us -> 80.7 us (1.023)
  Pallas kernels: 74.2 us -> 76 us
    pallas_call x1, Pallas kernels: 74.2 us -> 76 us  [layer(): pl.pallas_call(functools.partial(layer_kernel, ny, nx), out_shape=(jax.Sh...]
where the time goes in v4:
time: 80.7 us; the launch traced here: 80.6 us
  Pallas kernels  76 us (94%)
  local copies, waits for them, and re-layouts  3.92 us (5%)
    pallas_call x1, Pallas kernels, layer(): pl.pallas_call(functools.partial(layer_kernel, ny, nx), out_shape=(jax.Sh...  76 us
    unnamed x5, local copies, waits for them, and re-layouts  3.92 us

profile of v4, /device:TPU:97, one launch (start us, length us, event | category | flops | bytes accessed | tf_op | source)
XLA Modules:
  0.0 80.6 jit_solution(18123165351572062369)
XLA Ops:
  0.6 0.0 copy-start
  0.6 0.6 copy-done
  1.3 76.0 %layer.1 = (bf16[8,32,8192]{2,1,0:T(8,128)(2,1)S(1)}, bf16[32,8,128]{2,1,0:T(8,128)(2,1)S(1)}, bf16[32,8,128]{2,1,0:T(8,128)(2,1)S(1)}) custom-call(bf16[256,8192]{1,0:T(8,128)(2,1)} %tok_ref.1, bf16[8192,256]{1,0:T(8,128)(2,1)} %wq_ref.1, bf16[8192,1024]{1,0:T(8,128)(2,1)} %wk_ref.1, bf16[8192,1024]{1,0:T(8,128)(2,1)} %wv_ref.1, bf16[256,8192]{1,0:T(8,128)(2,1)} %wo_ref.1, ...), custom_call_target="tpu_custom_call" | custom-call | tf_op jit(solution)/shard_map/layer/pallas_call | solution.py:442
  77.3 2.0 %copy.14 = bf16[256,8192]{1,0:T(8,128)(2,1)} copy(bf16[256,8192]{1,0:T(8,128)(2,1)S(1)} %bitcast.1) | data formatting | bytes 8388608
  79.4 0.6 copy.15
  80.0 0.6 copy.16
Async XLA Ops:
  0.6 0.7 copy-start

commit v5 on v3

--- a/solution.py
+++ b/solution.py
@@ -12,6 +12,7 @@
 CHUNK_K = 8
 SLOTS = 16
 SEQS = 4
+AHEAD = 4
 
 
 def layer_kernel(ny, nx, tok_ref, wq_ref, wk_ref, wv_ref, wo_ref, kc_ref, vc_ref, len_ref,
@@ -73,22 +74,29 @@
         ks = pl.ds(i * kc, kc)
         copies["x", i] = pltpu.make_async_copy(tok_ref.at[:, ks], x_buf.at[:, ks], x_sem.at[i])
         copies["q", i] = pltpu.make_async_copy(wq_ref.at[ks], wq_buf.at[ks], wq_sem.at[i])
-        copies["x", i].start()
-        copies["q", i].start()
+        copies["k", i] = pltpu.make_async_copy(wk_ref.at[ks, kv_here], wkv_buf.at[ks, 0:kv_cols], wk_sem.at[i])
+        copies["v", i] = pltpu.make_async_copy(wv_ref.at[ks, kv_here], wkv_buf.at[ks, kv_cols:2 * kv_cols], wv_sem.at[i])
 
     def cache_copies(b, slot):
         gs = pl.ds(y * groups, groups)
         return (pltpu.make_async_copy(kc_ref.at[b, gs], k_buf.at[slot], k_sem.at[slot]),
                 pltpu.make_async_copy(vc_ref.at[b, gs], v_buf.at[slot], v_sem.at[slot]))
 
+    reads = [(copies["x", i], copies["q", i]) for i in range(CHUNK_K)] + [(copies["k", i], copies["v", i]) for i in range(CHUNK_K)]
+    reads += [cache_copies(b, b) for b in range(SLOTS)]
+
+    def read_next(n):
+        for pair in reads[:n]:
+            for copy in pair:
+                copy.start()
+        del reads[:n]
+
+    read_next(AHEAD)
     for i in range(CHUNK_K):
         ks = pl.ds(i * kc, kc)
         copies["x", i].wait()
         copies["q", i].wait()
-        copies["k", i] = pltpu.make_async_copy(wk_ref.at[ks, kv_here], wkv_buf.at[ks, 0:kv_cols], wk_sem.at[i])
-        copies["v", i] = pltpu.make_async_copy(wv_ref.at[ks, kv_here], wkv_buf.at[ks, kv_cols:2 * kv_cols], wv_sem.at[i])
-        copies["k", i].start()
-        copies["v", i].start()
+        read_next(1)
         prod = jnp.dot(x_buf[:, ks], wq_buf[ks, :], preferred_element_type=jnp.float32)
         acc_q[...] = prod if i == 0 else acc_q[...] + prod
     q_send[...] = acc_q[...].astype(jnp.bfloat16).reshape(nm, rows, hl * head)
@@ -103,9 +111,7 @@
         ks = pl.ds(i * kc, kc)
         copies["k", i].wait()
         copies["v", i].wait()
-        for b in range(i * SLOTS // CHUNK_K, (i + 1) * SLOTS // CHUNK_K):
-            for copy in cache_copies(b, b):
-                copy.start()
+        read_next(1)
         prod = jnp.dot(x_buf[mine, ks], wkv_buf[ks, :], preferred_element_type=jnp.float32)
         acc_kv[...] = prod if i == 0 else acc_kv[...] + prod
     kv_bf = acc_kv[...].astype(jnp.bfloat16)
@@ -124,6 +130,7 @@
     own_w.start()
     remote(wo_ref.at[:, other_cols], w_buf.at[my_rows], w_sem.at[0], w_sem.at[1], partner)
 
+    read_next(len(reads))
     for s in range(1, nm):
         arrive(q_recv.at[lax.rem(model + s, nm)], sem_q.at[1, s])
     for src in range(nm):
@@ -360,18 +367,18 @@
     attend(1)
     s0(0)
     attend(2)
+    s0(1)
     s1(0)
-    s0(1)
     attend(3)
+    s0(2)
     s1(1)
-    s0(2)
-    new_rows()
+    s0(3)
     s1(2)
-    s0(3)
     s1(3)
     s2()
     s3()
     s4()
+    new_rows()
     s5()
     s6()
     s7()

time: 78.9 us -> 76.7 us (0.972)
  Pallas kernels: 74.2 us -> 72 us
    pallas_call x1, Pallas kernels: 74.2 us -> 72 us  [layer(): pl.pallas_call(functools.partial(layer_kernel, ny, nx), out_shape=(jax.Sh...]
where the time goes in v5:
time: 76.7 us; the launch traced here: 76.6 us
  Pallas kernels  72 us (94%)
  local copies, waits for them, and re-layouts  3.92 us (5%)
    pallas_call x1, Pallas kernels, layer(): pl.pallas_call(functools.partial(layer_kernel, ny, nx), out_shape=(jax.Sh...  72 us
    unnamed x5, local copies, waits for them, and re-layouts  3.92 us

profile of v5, /device:TPU:97, one launch (start us, length us, event | category | flops | bytes accessed | tf_op | source)
XLA Modules:
  0.0 76.6 jit_solution(9052690230184042390)
XLA Ops:
  0.6 0.0 copy-start
  0.6 0.6 copy-done
  1.3 72.0 %layer.1 = (bf16[8,32,8192]{2,1,0:T(8,128)(2,1)S(1)}, bf16[32,8,128]{2,1,0:T(8,128)(2,1)S(1)}, bf16[32,8,128]{2,1,0:T(8,128)(2,1)S(1)}) custom-call(bf16[256,8192]{1,0:T(8,128)(2,1)} %tok_ref.1, bf16[8192,256]{1,0:T(8,128)(2,1)} %wq_ref.1, bf16[8192,1024]{1,0:T(8,128)(2,1)} %wk_ref.1, bf16[8192,1024]{1,0:T(8,128)(2,1)} %wv_ref.1, bf16[256,8192]{1,0:T(8,128)(2,1)} %wo_ref.1, ...), custom_call_target="tpu_custom_call" | custom-call | tf_op jit(solution)/shard_map/layer/pallas_call | solution.py:409
  73.3 2.0 %copy.14 = bf16[256,8192]{1,0:T(8,128)(2,1)} copy(bf16[256,8192]{1,0:T(8,128)(2,1)S(1)} %bitcast.1) | data formatting | bytes 8388608
  75.3 0.6 copy.15
  75.9 0.6 copy.16
Async XLA Ops:
  0.6 0.7 copy-start
